TPU v7x, 256 devices: a 2x2x32 block of a 4x8x32 slice. The times are simulated.
256 devices in a mesh: groups: 4 (over x, y), space: 64 (over z, core).
Axes of the slice: x: 2, y: 2, z: 32, core: 2. Of those that a mesh axis runs over, the one named last changes fastest.
The devices are a block of a 4x8x32 slice.
Arguments:
- hidden: bfloat16 [32768, 512], P(('groups', 'space')), parts along dimension 0, may hold values from -130 to 130
- norm_gain: float32 [512], replicated, may hold values from 0.5 to 2
- norm_shift: float32 [512], replicated, may hold values from -3 to 3
- conv_weight: bfloat16 [3, 3, 3, 512, 512], P(None, None, None, 'space'), may hold values from -0.0546875 to 0.0546875
- conv_bias: bfloat16 [512], replicated, may hold values from -3 to 3
Outputs:
- decoded: bfloat16 [16, 32, 256, 512], P('groups', None, 'space'), parts along dimension 0
There are 4 independent parts, one for each index of `groups`. A program takes and returns all parts, laid end to end along the dimension named above; an argument that names none is the same for every part. Nothing has to cross between parts.
All inputs are finite; a program needn't handle non-finite values.
Results may differ from a plain program's by a relative error of at most 0.0045.
Values may be sent and summed in bfloat16 or wider, within the bound.
A program may use at most 64 MiB of HBM per device.

v0:
```python
import jax
import jax.numpy as jnp
from jax import lax
from jax.sharding import Mesh
from jax.sharding import PartitionSpec as P

CHANNELS = 512
GROUPS = 32
FRAMES = 4
ROWS = 16
COL_DEV = 2
SPACE = ("space_0", "space_1")
GROUPS_SPACE = ("groups", "space_0", "space_1")


EPSILON = 1e-06


def one_axis_at_a_time(x, axes):
    for axis in axes:
        x = lax.psum(x, axis)
    return x


def with_halo(x, sides, width):
    for axis, dim in sides:
        size, length = (lax.axis_size(axis), x.shape[dim])
        up = [(i, (i + 1) % size) for i in range(size - 1)]
        down = [(j, i) for i, j in up]
        last = lax.slice_in_dim(x, length - width, length, axis=dim)
        first = lax.slice_in_dim(x, 0, width, axis=dim)
        before = lax.ppermute(last, axis, up)
        after = lax.ppermute(first, axis, down)
        x = jnp.concatenate([before, x, after], axis=dim)
    return x


def group_moments(values, population):
    grouped = values.reshape(-1, GROUPS, CHANNELS // GROUPS).astype(jnp.float32)
    totals, squares = (
        one_axis_at_a_time(jnp.sum(grouped, axis=(0, 2)), SPACE),
        one_axis_at_a_time(jnp.sum(grouped * grouped, axis=(0, 2)), SPACE),
    )
    average = totals / population
    spread = squares / population - average * average
    return (average, spread)


def shards(hidden, norm_gain, norm_shift, conv_weight, conv_bias):
    devices = lax.axis_size(SPACE)
    rows_dev = hidden.shape[0] // (COL_DEV * devices)
    population = float(FRAMES * ROWS * COL_DEV * devices * (CHANNELS // GROUPS))
    layout = hidden.reshape(rows_dev, devices * COL_DEV, CHANNELS)
    tile_cells = lax.all_to_all(layout, SPACE, split_axis=1, concat_axis=0, tiled=True)
    average, spread = group_moments(tile_cells, population)
    scaled = tile_cells.astype(jnp.float32).reshape(
        FRAMES, ROWS, COL_DEV, GROUPS, CHANNELS // GROUPS
    )
    scaled = (scaled - average[:, None]) * lax.rsqrt(spread + EPSILON)[:, None]
    normed = scaled.reshape(FRAMES, ROWS, COL_DEV, CHANNELS) * norm_gain + norm_shift
    active = jax.nn.silu(normed).astype(jnp.bfloat16)
    widened = with_halo(active, ((SPACE, 2),), 1)
    position = lax.axis_index(SPACE)
    lefthand = jnp.where(position == 0, active[:, :, :1], widened[:, :, :1])
    righthand = jnp.where(position == devices - 1, active[:, :, -1:], widened[:, :, -1:])
    widened = jnp.concatenate([lefthand, active, righthand], axis=2)
    doubled = jnp.repeat(jnp.repeat(widened, 2, axis=1), 2, axis=2)[:, :, 1:-1]
    padded = jnp.pad(doubled, ((2, 0), (1, 1), (0, 0), (0, 0)), mode="edge")
    initial = jnp.zeros((FRAMES, 2 * ROWS, 2 * COL_DEV, CHANNELS), jnp.float32)
    product = lax.conv_general_dilated(
        padded[None],
        lax.all_gather(conv_weight, SPACE, axis=3, tiled=True),
        (1, 1, 1),
        "VALID",
        dimension_numbers=("NDHWC", "DHWIO", "NDHWC"),
        preferred_element_type=jnp.float32,
    )
    summed = initial + product[0]
    return (summed + conv_bias.astype(jnp.float32)).astype(jnp.bfloat16)


def solution(mesh):
    torus = Mesh(
        mesh.devices.reshape(mesh.shape["groups"], 32, 2), ("groups", "space_0", "space_1")
    )
    return jax.shard_map(
        shards,
        mesh=torus,
        in_specs=(P(GROUPS_SPACE, None), P(), P(), P(None, None, None, SPACE, None), P()),
        out_specs=P("groups", None, SPACE, None),
        check_vma=False,
    )
```

profile of v0, /device:TPU:37, one launch (start us, length us, event | category | flops | bytes accessed | tf_op | source)
XLA Modules:
  0.0 228.4 jit_solution(5131043434642010950)
XLA Ops:
  6.5 0.0 copy-start.1
  6.5 0.0 copy-start
  6.6 0.0 copy-start.2
  6.6 0.0 all-gather.2.cloned.1.call-start
  6.6 0.7 all-gather.2.cloned.1.call-update
  7.3 1.1 copy.33
  8.4 0.5 broadcast.35
  8.9 1.4 reduce.6
  10.4 0.1 reshape.40
  10.4 65.5 %all_to_all.4 = bf16[64,2,512]{2,1,0:T(2,128)(2,1)S(1)} all-to-all(bf16[64,2,512]{2,1,0:T(2,128)(2,1)S(1)} %reshape.40), channel_id=1, replica_groups=mesh['groups'=4,'space_0'=32,'space_1'=2] {'space_0','space_1'}, dimensions={0} | all-to-all | bytes 262144 | tf_op jit(solution)/shard_map/all_to_all | solution.py:54
  75.9 0.1 reshape.41
  76.0 1.0 convert_reduce_fusion
  77.0 0.1 reduce_sum.24
  77.0 0.1 reduce_sum.36
  77.1 0.1 reduce_sum.25
  77.2 0.1 reduce_sum.37
  77.4 43.2 %all-reduce = (f32[32]{0:T(128)S(1)}, f32[32]{0:T(128)S(1)}) all-reduce(f32[32]{0:T(128)S(1)} %reduce_sum.37, f32[32]{0:T(128)S(1)} %reduce_sum.25), channel_id=1, replica_groups=mesh['groups'=4,'space_0'=32,'space_1'=2] {'space_0'}, use_global_device_ids=true, to_apply=%region_6.7 | all-reduce | flops 64 | bytes 512 | tf_op jit(solution)/shard_map/psum | solution.py:21
  120.6 14.5 %all-reduce.1 = (f32[32]{0:T(128)S(1)}, f32[32]{0:T(128)S(1)}) all-reduce(f32[32]{0:T(128)S(1)} %get-tuple-element.8, f32[32]{0:T(128)S(1)} %get-tuple-element.9), channel_id=1, replica_groups=mesh['groups'=4,'space_0'=32,'space_1'=2] {'space_1'}, use_global_device_ids=true, to_apply=%region_7.8 | all-reduce | flops 64 | bytes 512 | tf_op jit(solution)/shard_map/psum | solution.py:21
  135.1 0.1 mul.38
  135.2 0.1 mul.39
  135.3 0.1 sub.16
  135.3 0.1 sub.17
  135.4 0.2 reshape.38
  135.6 0.0 copy-done.1
  135.6 0.0 copy-done
  135.6 0.1 multiply_convert_fusion
  135.7 3.1 %collective-permute-start = (bf16[4,16,1,512]{3,1,2,0:T(8,128)(2,1)S(1)}, bf16[4,16,1,512]{3,1,2,0:T(8,128)(2,1)S(1)}, u32[]{:S(2)}, u32[]{:S(2)}) collective-permute-start(bf16[4,16,1,512]{3,1,2,0:T(8,128)(2,1)S(1)} %get-tuple-element.14), channel_id=1, source_target_pairs={{0,1},{1,2},{2,3},{3,4},{4,5},{5,6},{6,7},{7,8},{8,9},{9,10},{10,1... | collective-permute-start | bytes 196616 | tf_op jit(solution)/shard_map/ppermute | solution.py:32
  138.8 2.0 collective-permute-start.1
  140.8 0.0 copy-done.2
  140.8 0.0 collective-permute-done
  140.8 4.8 %collective-permute-done.1 = bf16[4,16,1,512]{3,1,2,0:T(8,128)(2,1)S(1)} collective-permute-done((bf16[4,16,1,512]{3,1,2,0:T(8,128)(2,1)S(1)}, bf16[4,16,1,512]{3,1,2,0:T(8,128)(2,1)S(1)}, u32[]{:S(2)}, u32[]{:S(2)}) %collective-permute-start.1) | collective-permute-done | bytes 65568 | tf_op jit(solution)/shard_map/ppermute | solution.py:33
  145.6 0.4 broadcast_in_dim.14
  146.1 0.2 reshape.35
  146.3 0.1 broadcast_in_dim.15
  146.4 0.1 slice.36
  146.5 0.6 fusion.9
  147.2 30.7 %all-gather.2.cloned.1.call-done = bf16[3,3,3,512,512]{4,3,2,1,0:T(8,128)(2,1)} async-done(((bf16[3,3,3,8,512]{4,3,2,1,0:T(8,128)(2,1)}), bf16[3,3,3,512,512]{4,3,2,1,0:T(8,128)(2,1)}) %all-gather.2.cloned.1.call-update) | async-done | bytes 14155792 | tf_op jit(solution)/shard_map/all_gather | solution.py:72
  177.9 42.6 %fusion.4 = f32[1,4,32,4,512]{4,0,3,2,1:T(1,128)S(1)} fusion(bf16[3,3,3,512,512]{4,3,2,1,0:T(8,128)(2,1)} %all-gather.2.cloned.1.call-done, bf16[1,6,34,6,512]{4,2,3,1,0:T(8,128)(2,1)S(1)} %fusion.9), kind=kOutput, calls=%fused_computation.6 | convolution fusion | flops 7247757312 | bytes 16457728 | tf_op jit(solution)/shard_map/conv_general_dilated | solution.py:70
  220.5 1.1 fusion.11
  (7 shorter events, 0.1 us)
Async XLA Ops:
  6.5 129.0 %copy-start.1 = (f32[512]{0:T(512)S(1)}, f32[512]{0:T(512)}, u32[]{:S(2)}) copy-start(f32[512]{0:T(512)} %param.6) | copy-start | bytes 6148
  6.5 129.1 %copy-start = (f32[512]{0:T(512)S(1)}, f32[512]{0:T(512)}, u32[]{:S(2)}) copy-start(f32[512]{0:T(512)} %param.7) | copy-start | bytes 6148
  6.6 134.2 %copy-start.2 = (bf16[512]{0:T(512)(128)(2,1)S(1)}, bf16[512]{0:T(512)(128)(2,1)}, u32[]{:S(2)}) copy-start(bf16[512]{0:T(512)(128)(2,1)} %param.9) | copy-start | bytes 3076
  6.6 171.3 %all-gather.2.cloned.1.call-start = ((), (), s32[]{:S(2)}) async-start(), calls=%async_computation.1 | async-start | bytes 14376960 | tf_op jit(solution)/shard_map/all_gather | solution.py:72
  135.7 5.1 %collective-permute-start = (bf16[4,16,1,512]{3,1,2,0:T(8,128)(2,1)S(1)}, bf16[4,16,1,512]{3,1,2,0:T(8,128)(2,1)S(1)}, u32[]{:S(2)}, u32[]{:S(2)}) collective-permute-start(bf16[4,16,1,512]{3,1,2,0:T(8,128)(2,1)S(1)} %get-tuple-element.14), channel_id=1, source_target_pairs={{0,1},{1,2},{2,3},{3,4},{4,5},{5,6},{6,7},{7,8},{8,9},{9,10},{10,1... | collective-permute-start | bytes 196616 | tf_op jit(solution)/shard_map/ppermute | solution.py:32
  138.8 6.8 %collective-permute-start.1 = (bf16[4,16,1,512]{3,1,2,0:T(8,128)(2,1)S(1)}, bf16[4,16,1,512]{3,1,2,0:T(8,128)(2,1)S(1)}, u32[]{:S(2)}, u32[]{:S(2)}) collective-permute-start(bf16[4,16,1,512]{3,1,2,0:T(8,128)(2,1)S(1)} %get-tuple-element.15), channel_id=1, source_target_pairs={{1,0},{2,1},{3,2},{4,3},{5,4},{6,5},{7,6},{8,7},{9,8},{10,9},{11,1... | collective-permute-start | bytes 196616 | tf_op jit(solution)/shard_map/ppermute | solution.py:33
Sparse Core Ops, SparseCore 0:
  9.2 168.6 all-gather.1
where the time goes:
time: 229 us; the launch traced here: 228 us
  blocking collectives  123 us (54%)
  matrix products  42.6 us (19%)
  waiting for transfers between devices  36.2 us (16%)
  between operations  13.6 us (6%)
  starting transfers between devices  5.03 us (2%)
  other arithmetic  4.5 us (2%)
  local copies, waits for them, and re-layouts  3.27 us (1%)
    all_to_all x1, blocking collectives, shards(): lax.all_to_all(layout, SPACE, split_axis=1, concat_axis=0, tiled=True)  65.5 us
    psum x2, blocking collectives, one_axis_at_a_time(): x = lax.psum(x, axis)  57.7 us
    conv_general_dilated x1, matrix products, shards(): lax.conv_general_dilated(padded[None], lax.all_gather(conv_weight, SPACE,...  42.6 us
    all_gather x1, waiting for transfers between devices, shards(): lax.all_gather(conv_weight, SPACE, axis=3, tiled=True)  30.7 us
    ppermute x1, waiting for transfers between devices, with_halo(): after = lax.ppermute(first, axis, down)  4.75 us
  transfers between devices with their start and end apart: 3, of which 2 were waited for; matrix products, arithmetic and copies ran while one was open for 3% of the time, Pallas kernels for 0%

commit v1 on v0

v1 whole, which is shorter than its diff:
```python
import functools

import jax
import jax.numpy as jnp
from jax import lax
from jax.experimental import pallas as pl
from jax.experimental.pallas import tpu as pltpu
from jax.sharding import PartitionSpec as P

GROUP = 16
FRAMES = 4
ROWS = 16
LANES = 128
TEAM = 4
TAPS = 9
EPSILON = 1e-6
MIB = 1 << 20

DMA = pltpu.SemaphoreType.DMA
F32, BF16 = jnp.float32, jnp.bfloat16
SHIFTS = [(0, 0), (0, -1), (0, 1), (-1, 0), (1, 0), (-1, -1), (-1, 1), (1, -1), (1, 1)]


def phases_of(dr, dc):
    rows = {-1: (0,), 0: (0, 1), 1: (1,)}
    return [(a, b) for a in rows[dr] for b in rows[dc]]


COLUMNS = [(s, p) for s in SHIFTS for p in phases_of(*s)]


def remote(src, dst, send, recv, device):
    return pltpu.make_async_remote_copy(
        src_ref=src, dst_ref=dst, send_sem=send, recv_sem=recv,
        device_id=device, device_id_type=pl.DeviceIdType.MESH,
    )


def signal(sem, device):
    pl.semaphore_signal(sem, inc=1, device_id=device, device_id_type=pl.DeviceIdType.MESH)


def wait_bytes(ref, sem):
    pltpu.make_async_copy(ref, ref, sem).wait()


def team(ny):
    g = lax.axis_index("groups")
    x, y = g // ny, g % ny
    x0, y0 = x - x % 2, y - y % 2
    return (x % 2) * 2 + y % 2, lambda p: (x0 + p // 2) * ny + y0 + p % 2


def group_matrix():
    lane = lax.broadcasted_iota(jnp.int32, (LANES, LANES), 0)
    packed = lax.broadcasted_iota(jnp.int32, (LANES, LANES), 1)
    return jnp.where(lane // GROUP == packed % 8, 1.0, 0.0).astype(F32)


def packed_mask(which):
    row = lax.broadcasted_iota(jnp.int32, (8, LANES), 0)
    lane = lax.broadcasted_iota(jnp.int32, (8, LANES), 1)
    return (lane // 32 == which) & ((lane // 8) % 4 == row % 4)


def hdot(a, b):
    return jnp.dot(a, b, preferred_element_type=F32, precision=lax.Precision.HIGHEST)


def pack(sums, which):
    return jnp.sum(jnp.where(packed_mask(which), hdot(sums, group_matrix()), 0.0), axis=0, keepdims=True)


def unpack(row, which):
    spread = jnp.where(packed_mask(which), jnp.broadcast_to(row, (8, LANES)), 0.0)
    return hdot(spread, group_matrix().T)


def exchange(ny, nd, x_ref, wq_ref, w, acts, totals, xs, stats, row, tot,
             local, ringsend, ringrecv, give, giverecv, own, ask, a2asend, a2arecv,
             statsend, statrecv, partsend, partrecv, totsend, totrecv):
    me = lax.axis_index("space")
    z, c = me // 2, me % 2
    nz = nd // 2
    half = nz // 2
    near = max(1, nz // 8)
    q, group_at = team(ny)

    def at(zz, core):
        return {"space": lax.rem(zz + 2 * nz, nz) * 2 + core}

    sibling = {"space": z * 2 + 1 - c}
    barrier = pltpu.get_barrier_semaphore()

    @pl.when(c == 1)
    def _():
        signal(barrier, at(z + 1, 1))
        signal(barrier, at(z - 1, 1))
        signal(barrier, sibling)
        load = pltpu.make_async_copy(wq_ref.at[:, :, :, pl.ds(q * LANES, LANES)], w.at[:, me], local.at[0])
        load.start()
        pl.semaphore_wait(barrier, 3)
        mine = remote(x_ref, xs.at[:, 1], own.at[0, 0], own.at[1, 0], sibling)
        mine.start()
        load.wait()

        def piece(zz, j):
            return w.at[j, pl.ds(lax.rem(zz + 2 * nz, nz) * 2, 2)]

        def right(p, s, j):
            return remote(p, p, ringsend.at[0], ringrecv.at[0, s, j], at(z + 1, 1))

        def left(p, s, j):
            return remote(p, p, ringsend.at[1], ringrecv.at[1, s, j], at(z - 1, 1))

        for j in range(3):
            theirs = w.at[j, z * 2]
            remote(theirs, theirs, own.at[0, 1 + j], own.at[1, 1 + j], sibling).wait_recv()
            p = piece(z, j)
            right(p, 0, j).start()
            left(p, 0, j).start()
            m = w.at[j, me]
            remote(m, m, give, giverecv, sibling).start()

        @pl.loop(0, half)
        def _(s):
            for j in range(3):
                p = piece(z - s - 1, j)
                right(p, s, j).wait_recv()

                @pl.when(s < half - 1)
                def _():
                    right(p, s + 1, j).start()

                remote(p, p, give, giverecv, sibling).start()

                @pl.when(s < half - 1)
                def _():
                    o = piece(z + s + 1, j)
                    left(o, s, j).wait_recv()

                    @pl.when(s < half - 2)
                    def _():
                        left(o, s + 1, j).start()

                    remote(o, o, give, giverecv, sibling).start()

        mine.wait_send()
        for p in range(TEAM):
            remote(acts.at[p], acts.at[p], partsend.at[1], partrecv.at[1, p], sibling).wait_recv()
        remote(totals, totals, totsend.at[1], totrecv.at[1], sibling).wait_recv()
        wait_bytes(w.at[:, pl.ds(0, 2 * half)], ringsend.at[0])
        wait_bytes(w.at[:, pl.ds(0, 2 * half - 2)], ringsend.at[1])
        wait_bytes(w.at[:, pl.ds(0, nd - 1)], give)

    @pl.when(c == 0)
    def _():
        for d in range(1, near + 1):
            signal(barrier, at(z + d, 0))
            signal(barrier, at(z - d, 0))
        for k in range(1, TEAM):
            signal(barrier, {"groups": group_at((q + k) % TEAM)})
        signal(barrier, sibling)
        load = pltpu.make_async_copy(wq_ref.at[:, :, :, pl.ds(q * LANES, LANES)], w.at[:, me], local.at[0])
        load.start()
        mine = pltpu.make_async_copy(x_ref, xs.at[:, 0], local.at[1])
        mine.start()
        pl.semaphore_wait(barrier, 2 * near + TEAM)
        cover, k = near, 0
        if cover < half:
            signal(ask.at[k], at(z + near, 0))
            signal(ask.at[k], at(z - near, 0))
        load.wait()
        pieces = []
        for j in range(3):
            p = w.at[j, me]
            pieces.append(remote(p, p, own.at[0, 1 + j], own.at[1, 1 + j], sibling))
            pieces[-1].start()
        mine.wait()
        remote(x_ref, xs.at[:, 1], own.at[0, 0], own.at[1, 0], sibling).wait_recv()

        def summed(f):
            def body(i, acc):
                out = []
                for r in range(2):
                    v = xs[i, r].astype(F32).reshape(3, 8, LANES)
                    out.append(f(v))
                return acc + out[0] + out[1]
            acc = lax.fori_loop(0, nz, body, jnp.zeros((3, 8, LANES), F32))
            rows = lax.broadcasted_iota(jnp.int32, (8, LANES), 0)
            return jnp.where(rows >= 4, acc[0], 0.0) + acc[1] + jnp.where(rows < 4, acc[2], 0.0)

        count = float(2 * 4 * nz * GROUP)
        first = pack(summed(lambda v: v), 0)
        mean = unpack(first, 0) * (1.0 / count)
        second = pack(summed(lambda v: (v - mean[None]) ** 2), 1)
        row[...] = first + second

        while cover < half:
            pl.semaphore_wait(ask.at[k], 2)
            cover, k = cover + near, k + 1
            if cover < half:
                signal(ask.at[k], at(z + near, 0))
                signal(ask.at[k], at(z - near, 0))

        def send(d, batch):
            zz = lax.rem(z + d + 2 * nz, nz)
            remote(row, stats.at[z], statsend, statrecv, at(zz, 0)).start()
            remote(xs.at[zz], acts.at[q, z], a2asend, a2arecv.at[batch], at(zz, 0)).start()

        send(half, (half - 1) // near)

        @pl.loop(1, half)
        def _(i):
            d = half - i
            batch = (d - 1) // near
            send(d, batch)
            send(-d, batch)

        def share(zz, src, batch):
            for k in range(1, TEAM):
                remote(src, acts.at[q, zz], partsend.at[0], partrecv.at[0, batch],
                       {"groups": group_at((q + k) % TEAM)}).start()

        acts[q, z] = xs[z]
        stats[z] = row[...]
        batches = (half + near - 1) // near
        share(z, xs.at[z], 0)
        sizes = [2 * near] * batches
        sizes[-1] = nz - 1 - 2 * near * (batches - 1)
        for b in range(batches):
            wait_bytes(acts.at[0, pl.ds(0, sizes[b])], a2arecv.at[b])

            @pl.loop(b * near + 1, min((b + 1) * near, half - 1) + 1)
            def _(d):
                for zz in (lax.rem(z + d, nz), lax.rem(z - d + nz, nz)):
                    share(zz, acts.at[q, zz], b)

            if b == batches - 1:
                zz = lax.rem(z + half, nz)
                share(zz, acts.at[q, zz], b)
            if b == 0:
                pass
            if b == batches - 1:
                remote(acts.at[q], acts.at[q], partsend.at[1], partrecv.at[1, q], sibling).start()

        wait_bytes(stats.at[pl.ds(0, nz - 1)], statrecv)
        every = stats[...].reshape(nz, LANES)
        lane = lax.broadcasted_iota(jnp.int32, (nz, LANES), 1)
        mean = jnp.sum(every, axis=0, keepdims=True) * (1.0 / (count * nz))
        off = jnp.where(lane < 32, (every * (1.0 / count) - mean) ** 2 * count, 0.0)
        spread = jnp.where(lane < 32, 0.0, every)
        spread = jnp.sum(spread + pltpu.roll(off, 32, 1), axis=0, keepdims=True) * (1.0 / (count * nz))
        tot[...] = jnp.where(lane[:1] < 32, mean, spread)
        totals[q] = tot[...]
        for k in range(1, TEAM):
            remote(tot, totals.at[q], totsend.at[0], totrecv.at[0],
                   {"groups": group_at((q + k) % TEAM)}).start()
        wait_bytes(totals.at[pl.ds(0, TEAM - 1)], totrecv.at[0])
        remote(totals, totals, totsend.at[1], totrecv.at[1], sibling).start()

        for b in range(batches):
            n = sizes[b] + (1 if b == 0 else 0)
            wait_bytes(acts.at[pl.ds(0, TEAM - 1), pl.ds(0, n)], partrecv.at[0, b])
        for k in range(1, TEAM):
            p = lax.rem(q + k, TEAM)
            remote(acts.at[p], acts.at[p], partsend.at[1], partrecv.at[1, p], sibling).start()

        wait_bytes(w.at[:, pl.ds(0, nd - 1)], giverecv)
        for p in pieces:
            p.wait_send()
        wait_bytes(stats.at[pl.ds(0, nz - 1)], statsend)
        wait_bytes(acts.at[0, pl.ds(0, nz - 1)], a2asend)
        wait_bytes(acts.at[pl.ds(0, TEAM - 1)], partsend.at[0])
        wait_bytes(acts, partsend.at[1])
        wait_bytes(totals.at[pl.ds(0, TEAM - 1)], totsend.at[0])
        wait_bytes(totals, totsend.at[1])


def convolve(ny, nd, w, acts, totals, gain, shift, bias, out, ys, a, mix, acc, total, turn):
    me = lax.axis_index("space")
    c = me % 2
    q, _ = team(ny)
    k_dim = a.shape[-1]

    for p in range(TEAM):
        mean = unpack(totals[p], 0)
        var = unpack(totals[p], 1)
        g = jnp.concatenate([gain[...], gain[...]], axis=0)
        b = jnp.concatenate([shift[...], shift[...]], axis=0)
        scale = g * lax.rsqrt(var + EPSILON)
        move = b - mean * scale

        @pl.loop(0, ROWS)
        def _(r):
            for f in range(FRAMES):
                v = acts[p, f * ROWS + r, pl.ds(pl.multiple_of(c * 8, 8), 16)].astype(F32).reshape(2, 8, LANES)
                v = v * scale[None] + move[None]
                v = v / (1.0 + jnp.exp(-v))
                ys[pl.ds(pl.multiple_of(r * 256 + (p * FRAMES + f) * 16, 16), 16)] = v.reshape(16, LANES)

    tiles = k_dim // LANES

    @pl.loop(0, ROWS)
    def _(r):
        for col in range(4):
            for t in range(tiles):
                v = ys[pl.ds(r * 256 + col * tiles + t, 16, stride=16)].astype(BF16)
                a[r + 1, col, :, t * LANES:(t + 1) * LANES] = v

    a[0] = a[1]
    a[ROWS + 1] = a[ROWS]

    row = lax.broadcasted_iota(jnp.int32, (8, LANES), 0) % FRAMES

    for dt in (2, 1, 0):
        @pl.loop(0, nd // 8)
        def _(i):
            tap = [w[dt, pl.ds(i * 8, 8), n].reshape(64, LANES).astype(F32) for n in range(TAPS)]

            def sums(x):
                return {(0, -1): x[0], (0, 0): x[1] + x[2], (1, 0): x[0] + x[1], (1, 1): x[2]}

            by_row = [sums([tap[n * 3 + e] for n in range(3)]) for e in range(3)]
            both = {k: sums([by_row[e][k] for e in range(3)]) for k in by_row[0]}
            for n, ((dr, dc), (pr, pc)) in enumerate(COLUMNS):
                mix[pl.ds(pl.multiple_of(i * 64, 64), 64), n * LANES:(n + 1) * LANES] = both[(pr, dr)][(pc, dc)].astype(BF16)

        dst = total if dt == 2 else acc
        at = 0
        for dr, dc in SHIFTS:
            ps = phases_of(dr, dc)
            lhs = a[1 + dr:1 + dr + ROWS, 1 + dc:3 + dc].reshape(2 * ROWS * 16, k_dim)
            r = jnp.dot(lhs, mix[:, at:at + len(ps) * LANES], preferred_element_type=F32)
            at += len(ps) * LANES
            if (dr, dc) == (0, 0):
                dst[...] = r
            else:
                for n, (pr, pc) in enumerate(ps):
                    cols = slice((pr * 2 + pc) * LANES, (pr * 2 + pc + 1) * LANES)
                    dst[:, cols] += r[:, n * LANES:(n + 1) * LANES]
        if dt != 2:
            back = 2 - dt

            @pl.loop(0, acc.shape[0] // 8)
            def _(i):
                rows = pl.ds(pl.multiple_of(i * 8, 8), 8)
                for n in range(4):
                    cols = slice(n * LANES, (n + 1) * LANES)
                    v = acc[rows, cols]
                    moved = jnp.where(row >= 1, pltpu.roll(v, 1, 0), v)
                    if back == 2:
                        moved = jnp.where(row >= 2, pltpu.roll(v, 2, 0), moved)
                    total[rows, cols] += moved

    bias_row = bias[q]
    for r in range(ROWS):
        for cc in range(2):
            for n in range(4):
                pr, pc = n // 2, n % 2
                turn[((r * 2 + pr) * 2 + cc) * 2 + pc] = total[(r * 2 + cc) * 16:(r * 2 + cc + 1) * 16, n * LANES:(n + 1) * LANES] + bias_row
    flat = turn.reshape(ROWS * 8 * 16, LANES)
    for p in range(TEAM):
        for f in range(FRAMES):
            out[p, f] = flat[pl.ds(p * FRAMES + f, ROWS * 8, stride=16)].astype(BF16)


def swap(ny, mine, out, send, recv):
    q, group_at = team(ny)
    barrier = pltpu.get_barrier_semaphore()
    for k in range(1, TEAM):
        signal(barrier, {"groups": group_at((q + k) % TEAM)})
    pl.semaphore_wait(barrier, TEAM - 1)
    for k in (3, 2, 1):
        p = lax.rem(q + k, TEAM)
        remote(mine.at[p], out.at[q], send, recv, {"groups": group_at(p)}).start()
    out[q] = mine[q]
    wait_bytes(out.at[pl.ds(0, TEAM - 1)], recv)
    wait_bytes(out.at[pl.ds(0, TEAM - 1)], send)


VMEM = pl.BlockSpec(memory_space=pltpu.VMEM)
ANY = pl.BlockSpec(memory_space=pl.ANY)


def shards(ny, hidden, norm_gain, norm_shift, conv_weight, conv_bias):
    nd = lax.axis_size("space")
    nz = nd // 2
    channels = hidden.shape[1]
    tiles = channels // LANES
    cols = hidden.shape[0] // nz
    near = max(1, nz // 8)
    batches = (nz // 2 + near - 1) // near
    h = hidden.reshape(nz, cols, channels)
    before = jnp.concatenate([h[:1, :1], h[:-1, -1:]], axis=0)
    after = jnp.concatenate([h[1:, :1], h[-1:, -1:]], axis=0)
    x6 = jnp.concatenate([before, h, after], axis=1).reshape(nz, (cols + 2) * tiles, LANES)
    wide = (cols + 2) * tiles
    cin = conv_weight.shape[3]
    wq = conv_weight.reshape(3, TAPS, cin, conv_weight.shape[4])
    w, acts, totals = pl.pallas_call(
        functools.partial(exchange, ny, nd),
        out_shape=(
            jax.ShapeDtypeStruct((3, nd, TAPS, cin, LANES), BF16),
            jax.ShapeDtypeStruct((TEAM, nz, 2, wide, LANES), BF16),
            jax.ShapeDtypeStruct((TEAM, 1, LANES), F32),
        ),
        in_specs=[ANY, ANY],
        out_specs=(VMEM, VMEM, VMEM),
        scratch_shapes=[
            pltpu.VMEM((nz, 2, wide, LANES), BF16),
            pltpu.VMEM((nz, 1, LANES), F32),
            pltpu.VMEM((1, LANES), F32),
            pltpu.VMEM((1, LANES), F32),
            DMA((2,)), DMA((2,)), DMA((2, nz // 2, 3)), DMA, DMA, DMA((2, 4)),
            pltpu.SemaphoreType.REGULAR((max(1, batches),)),
            DMA, DMA((batches,)), DMA, DMA, DMA((2,)), DMA((2, max(batches, TEAM))), DMA((2,)), DMA((2,)),
        ],
        compiler_params=pltpu.CompilerParams(collective_id=0, has_side_effects=True, vmem_limit_bytes=24 * MIB),
        name="exchange",
    )(x6, wq)
    mine = pl.pallas_call(
        functools.partial(convolve, ny, nd),
        out_shape=jax.ShapeDtypeStruct((TEAM, FRAMES, ROWS * 8, LANES), BF16),
        in_specs=[VMEM] * 6,
        out_specs=VMEM,
        scratch_shapes=[
            pltpu.VMEM((ROWS * 256, LANES), F32),
            pltpu.VMEM((ROWS + 2, 4, 16, channels), BF16),
            pltpu.VMEM((channels, 16 * LANES), BF16),
            pltpu.VMEM((2 * ROWS * 16, 4 * LANES), F32),
            pltpu.VMEM((2 * ROWS * 16, 4 * LANES), F32),
            pltpu.VMEM((ROWS * 8, 16, LANES), F32),
        ],
        compiler_params=pltpu.CompilerParams(vmem_limit_bytes=48 * MIB),
        name="convolve",
    )(w, acts.reshape(TEAM, nd, wide, LANES), totals, norm_gain.reshape(tiles, LANES),
      norm_shift.reshape(tiles, LANES), conv_bias.astype(F32).reshape(tiles, 1, LANES))
    parts = pl.pallas_call(
        functools.partial(swap, ny),
        out_shape=jax.ShapeDtypeStruct((TEAM, FRAMES, ROWS * 8, LANES), BF16),
        in_specs=[VMEM],
        out_specs=VMEM,
        scratch_shapes=[DMA, DMA],
        compiler_params=pltpu.CompilerParams(collective_id=1, has_side_effects=True),
        name="swap",
    )(mine)
    parts = parts.reshape(TEAM, FRAMES, ROWS * 2, 4, LANES)
    return jnp.transpose(parts, (1, 2, 3, 0, 4)).reshape(FRAMES, ROWS * 2, 4, channels)


def solution(mesh):
    ny = len({d.coords[1] for d in mesh.devices.flat})
    return jax.shard_map(
        functools.partial(shards, ny),
        mesh=mesh,
        in_specs=(P(("groups", "space"), None), P(), P(), P(None, None, None, "space", None), P()),
        out_specs=P("groups", None, "space", None),
        check_vma=False,
    )
```

time: 229 us -> 113 us (0.49)
  blocking collectives: 123 us -> 0 us
  Pallas kernels: 0 us -> 105 us
  matrix products: 42.6 us -> 0 us
  waiting for transfers between devices: 36.2 us -> 0 us
  between operations: 13.6 us -> 0.08 us
  starting transfers between devices: 5.03 us -> 0 us
  other arithmetic: 4.5 us -> 0.9 us
  local copies, waits for them, and re-layouts: 3.27 us -> 6.26 us
    pallas_call x0 -> x3, Pallas kernels: none -> 105 us  [the longest x1 83.2 us: shards(): pl.pallas_call(functools.partial(exchange, ny, nd), out_shape=(jax.ShapeD...]
    all_to_all x1 -> x0, blocking collectives: 65.5 us -> none  [shards(): lax.all_to_all(layout, SPACE, split_axis=1, concat_axis=0, tiled=True)]
    psum x2 -> x0, blocking collectives: 57.7 us -> none  [one_axis_at_a_time(): x = lax.psum(x, axis)]
    conv_general_dilated x1 -> x0, matrix products: 42.6 us -> none  [shards(): lax.conv_general_dilated(padded[None], lax.all_gather(conv_weight, SPACE,...]
    all_gather x1 -> x0, waiting for transfers between devices: 30.7 us -> none  [shards(): lax.all_gather(conv_weight, SPACE, axis=3, tiled=True)]
    ppermute x2 -> x0, starting transfers between devices: 5.02 us -> none  [the longest x1 3.07 us: with_halo(): before = lax.ppermute(last, axis, up)]
    ppermute x2 -> x0, waiting for transfers between devices: 4.75 us -> none  [the longest x1 4.75 us: with_halo(): after = lax.ppermute(first, axis, down)]
    unnamed x9 -> x8, local copies, waits for them, and re-layouts: 0.68 us -> 3.08 us
  transfers between devices with their start and end apart: 3 -> 0, of which waited for: 2 -> 0; matrix products, arithmetic and copies ran while one was open for 3% -> 0% of each run, Pallas kernels for 0% -> 0%
where the time goes in v1:
time: 113 us; the launch traced here: 112 us
  Pallas kernels  105 us (93%)
  local copies, waits for them, and re-layouts  6.26 us (6%)
    pallas_call x1, Pallas kernels, shards(): pl.pallas_call(functools.partial(exchange, ny, nd), out_shape=(jax.ShapeD...  83.2 us
    pallas_call x1, Pallas kernels, shards(): pl.pallas_call(functools.partial(convolve, ny, nd), out_shape=jax.ShapeDt...  11.2 us
    pallas_call x1, Pallas kernels, shards(): pl.pallas_call(functools.partial(swap, ny), out_shape=jax.ShapeDtypeStruc...  10.7 us
    unnamed x8, local copies, waits for them, and re-layouts  3.08 us

profile of v1, /device:TPU:37, one launch (start us, length us, event | category | flops | bytes accessed | tf_op | source)
XLA Modules:
  0.0 112.3 jit_solution(14900190907822703346)
XLA Ops:
  0.0 0.7 reshape.39
  0.7 0.9 reshape.29
  1.6 0.1 fusion.1
  1.7 0.2 maximum_maximum_fusion
  2.0 0.1 reshape.30.x_ref
  2.1 0.0 copy-start.1
  2.1 0.9 copy-done.1
  3.0 83.2 %exchange.1 = (bf16[3,64,9,8,128]{4,3,2,1,0:T(8,128)(2,1)S(1)}, bf16[4,32,2,24,128]{4,3,2,1,0:T(8,128)(2,1)S(1)}, f32[4,1,128]{2,1,0:T(1,128)S(1)}) custom-call(bf16[32,24,128]{2,1,0:T(8,128)(2,1)S(1)} %reshape.30.x_ref, bf16[3,9,8,512]{3,2,1,0:T(8,128)(2,1)S(1)} %bitcast.13), custom_call_target="tpu_custom_call" | custom-call | tf_op jit(solution)/shard_map/exchange/pallas_call | solution.py:401
  86.2 0.0 copy-start.2
  86.2 0.7 copy-done.2
  86.9 0.0 copy-start.3
  86.9 0.7 copy-done.3
  87.6 11.2 %convolve.1.mine = bf16[4,4,128,128]{3,2,1,0:T(8,128)(2,1)S(1)} custom-call(bf16[3,64,9,8,128]{4,3,2,1,0:T(8,128)(2,1)S(1)} %get-tuple-element.8.w, bf16[4,64,24,128]{3,2,1,0:T(8,128)(2,1)S(1)} %bitcast.12, f32[4,1,128]{2,1,0:T(1,128)S(1)} %get-tuple-element.10.totals, f32[4,128]{1,0:T(4,128)S(1)} %bitcast.15, f32[4,128]{1,0:T(4,128)S(1)} %bitcast.16, ...), custom_call_target="tpu_custom_call" | custom-call | tf_op jit(solution)/shard_map/convolve/pallas_call | solution.py:422
  98.8 0.0 copy-start
  98.8 0.8 copy-done
  99.6 10.7 %swap.1 = bf16[4,4,128,128]{3,2,1,0:T(8,128)(2,1)} custom-call(bf16[4,4,128,128]{3,2,1,0:T(8,128)(2,1)} %copy-done), custom_call_target="tpu_custom_call" | custom-call | tf_op jit(solution)/shard_map/swap/pallas_call | solution.py:439
  110.3 2.0 %copy.10 = bf16[4,4,32,1,4,128]{5,4,0,3,2,1:T(4,128)(2,1)} copy(bf16[4,4,32,1,4,128]{5,4,3,2,1,0:T(4,128)(2,1)} %bitcast.17) | data formatting | bytes 1048576 | tf_op jit(solution)/shard_map/reshape | solution.py:449
  (1 shorter events, 0.0 us)
Async XLA Ops:
  2.1 0.9 copy-start.1
  86.2 0.7 copy-start.2
  86.9 0.7 copy-start.3
  98.8 0.8 copy-start

commit v2 on v1

v2 whole, which is shorter than its diff:
```python
import functools

import jax
import jax.numpy as jnp
from jax import lax
from jax.experimental import pallas as pl
from jax.experimental.pallas import tpu as pltpu
from jax.sharding import PartitionSpec as P

GROUP = 16
FRAMES = 4
ROWS = 16
LANES = 128
TEAM = 4
TAPS = 9
EPSILON = 1e-6
MIB = 1 << 20
YROWS = 40
TROWS = 24

DMA = pltpu.SemaphoreType.DMA
F32, BF16 = jnp.float32, jnp.bfloat16
SHIFTS = [(0, 0), (0, -1), (0, 1), (-1, 0), (1, 0), (-1, -1), (-1, 1), (1, -1), (1, 1)]


def phases_of(dr, dc):
    rows = {-1: (0,), 0: (0, 1), 1: (1,)}
    return [(a, b) for a in rows[dr] for b in rows[dc]]


COLUMNS = [(s, p) for s in SHIFTS for p in phases_of(*s)]


def remote(src, dst, send, recv, device):
    return pltpu.make_async_remote_copy(
        src_ref=src, dst_ref=dst, send_sem=send, recv_sem=recv,
        device_id=device, device_id_type=pl.DeviceIdType.MESH,
    )


def signal(sem, device):
    pl.semaphore_signal(sem, inc=1, device_id=device, device_id_type=pl.DeviceIdType.MESH)


def wait_bytes(ref, sem):
    pltpu.make_async_copy(ref, ref, sem).wait()


def team(ny):
    g = lax.axis_index("groups")
    x, y = g // ny, g % ny
    x0, y0 = x - x % 2, y - y % 2
    return (x % 2) * 2 + y % 2, lambda p: (x0 + p // 2) * ny + y0 + p % 2


def group_matrix():
    lane = lax.broadcasted_iota(jnp.int32, (LANES, LANES), 0)
    packed = lax.broadcasted_iota(jnp.int32, (LANES, LANES), 1)
    return jnp.where(lane // GROUP == packed % 8, 1.0, 0.0).astype(F32)


def packed_mask(which):
    row = lax.broadcasted_iota(jnp.int32, (8, LANES), 0)
    lane = lax.broadcasted_iota(jnp.int32, (8, LANES), 1)
    return (lane // 32 == which) & ((lane // 8) % 4 == row % 4)


def hdot(a, b):
    return jnp.dot(a, b, preferred_element_type=F32, precision=lax.Precision.HIGHEST)


def pack(sums, which):
    return jnp.sum(jnp.where(packed_mask(which), hdot(sums, group_matrix()), 0.0), axis=0, keepdims=True)


def unpack(row, which):
    spread = jnp.where(packed_mask(which), jnp.broadcast_to(row, (8, LANES)), 0.0)
    return hdot(spread, group_matrix().T)


def rounds_of(half):
    known, steps = 1, []
    while known < half:
        step = min(known, max(1, half // 4))
        known += step
        steps.append((step, min(known, half)))
    return steps


def kernel(ny, nd, h_ref, wq_ref, gain, shift, bias, out,
           w, mix, acts, totals, raw, cells, flat, stats, row, tot, ys, a, acc, total, turn, mine,
           local, ringsend, ringrecv, give, giverecv, own, ask, a2asend, a2arecv,
           statsend, statrecv, partsend, partrecv, northsend, northrecv, totsend, totrecv, outsend, outrecv):
    me = lax.axis_index("space")
    z, c = me // 2, me % 2
    nz = nd // 2
    half = nz // 2
    q, group_at = team(ny)
    rounds = rounds_of(half)
    spans, last = [], 0
    for known in [1] + [r[1] for r in rounds]:
        spans.append((last + 1, known))
        last = known
    sizes = [2 * (hi - lo + 1) - (1 if hi == half else 0) for lo, hi in spans]

    def at(zz, core):
        return {"space": lax.rem(zz + 2 * nz, nz) * 2 + core}

    sibling = {"space": z * 2 + 1 - c}
    barrier = pltpu.get_barrier_semaphore()

    def blend(zz):
        zz = lax.rem(zz + 2 * nz, nz)
        for dt in range(3):
            tap = [w[dt, pl.ds(zz * 2, 2), n].reshape(16, LANES).astype(F32) for n in range(TAPS)]

            def sums(x):
                return {(0, -1): x[0], (0, 0): x[1] + x[2], (1, 0): x[0] + x[1], (1, 1): x[2]}

            by_row = [sums([tap[n * 3 + e] for n in range(3)]) for e in range(3)]
            both = {k: sums([by_row[e][k] for e in range(3)]) for k in by_row[0]}
            for n, ((dr, dc), (pr, pc)) in enumerate(COLUMNS):
                mix[dt, pl.ds(pl.multiple_of(zz * 16, 16), 16), n * LANES:(n + 1) * LANES] = both[(pr, dr)][(pc, dc)].astype(BF16)

    load = pltpu.make_async_copy(wq_ref.at[:, :, :, pl.ds(q * LANES, LANES)], w.at[:, me], local.at[0])
    rows_in = pltpu.make_async_copy(h_ref, raw.at[0], local.at[1])

    @pl.when(c == 1)
    def _():
        signal(barrier, at(z + 1, 1))
        signal(barrier, at(z - 1, 1))
        signal(barrier, sibling)
        load.start()
        rows_in.start()
        pl.semaphore_wait(barrier, 3)
        rows_in.wait()
        rows_out = remote(raw.at[0], raw.at[1], own.at[0, 0], own.at[1, 0], sibling)
        rows_out.start()
        load.wait()

        def piece(zz, j):
            return w.at[j, pl.ds(lax.rem(zz + 2 * nz, nz) * 2, 2)]

        def right(p, s, j):
            return remote(p, p, ringsend.at[0], ringrecv.at[0, s, j], at(z + 1, 1))

        def left(p, s, j):
            return remote(p, p, ringsend.at[1], ringrecv.at[1, s, j], at(z - 1, 1))

        for j in range(3):
            theirs = w.at[j, z * 2]
            remote(theirs, theirs, own.at[0, 1 + j], own.at[1, 1 + j], sibling).wait_recv()
            p = piece(z, j)
            right(p, 0, j).start()
            left(p, 0, j).start()
            m = w.at[j, me]
            remote(m, m, give, giverecv.at[half], sibling).start()
        blend(z)

        @pl.loop(0, half)
        def _(s):
            for j in range(3):
                p = piece(z - s - 1, j)
                right(p, s, j).wait_recv()

                @pl.when(s < half - 1)
                def _():
                    right(p, s + 1, j).start()

                remote(p, p, give, giverecv.at[s], sibling).start()

                @pl.when(s < half - 1)
                def _():
                    o = piece(z + s + 1, j)
                    left(o, s, j).wait_recv()

                    @pl.when(s < half - 2)
                    def _():
                        left(o, s + 1, j).start()

                    remote(o, o, give, giverecv.at[s], sibling).start()

            blend(z - s - 1)

            @pl.when(s < half - 1)
            def _():
                blend(z + s + 1)

        rows_out.wait_send()
        wait_bytes(w.at[:, pl.ds(0, 2 * half)], ringsend.at[0])
        wait_bytes(w.at[:, pl.ds(0, 2 * half - 2)], ringsend.at[1])
        wait_bytes(w.at[:, pl.ds(0, nd - 1)], give)
        wait_bytes(acts, northrecv)
        remote(totals, totals, totsend.at[1], totrecv.at[1], sibling).wait_recv()

    @pl.when(c == 0)
    def _():
        signal(barrier, at(z + 1, 0))
        signal(barrier, at(z - 1, 0))
        signal(barrier, sibling)
        for k in range(1, TEAM):
            signal(barrier, {"groups": group_at((q + k) % TEAM)})
        load.start()
        rows_in.start()
        pl.semaphore_wait(barrier, 2 + TEAM)

        def tell(k):
            if k < len(rounds):
                signal(ask.at[k], at(z + rounds[k][0], 0))
                signal(ask.at[k], at(z - rounds[k][0], 0))

        tell(0)
        load.wait()
        pieces = []
        for j in range(3):
            p = w.at[j, me]
            pieces.append(remote(p, p, own.at[0, 1 + j], own.at[1, 1 + j], sibling))
            pieces[-1].start()
        rows_in.wait()
        remote(raw.at[0], raw.at[1], own.at[0, 0], own.at[1, 0], sibling).wait_recv()

        wide = raw.shape[1]
        tiles = raw.shape[2] // LANES
        for r in range(2):
            for t in range(tiles):
                flat[pl.ds(r * tiles + t, wide, stride=8)] = raw[r, :, t * LANES:(t + 1) * LANES].astype(F32)
        x = flat[...].reshape(wide, 8, LANES)
        cells[pl.ds(1, wide)] = x.astype(BF16)
        cells[0] = x[0].astype(BF16)
        cells[wide + 1] = x[wide - 1].astype(BF16)

        def each(b, body):
            lo, hi = spans[b]

            @pl.loop(lo, min(hi, half - 1) + 1)
            def _(d):
                body(d)
                body(-d)

            if hi == half:
                body(half)

        def for_chip(zz):
            return cells.at[pl.ds(zz * 4, 6)]

        def send_rows(b):
            def body(d):
                zz = lax.rem(z + d + nz, nz)
                remote(for_chip(zz), acts.at[q, z], a2asend, a2arecv.at[b], at(zz, 0)).start()
            each(b, body)

        def send_stats(b):
            each(b, lambda d: remote(row, stats.at[z], statsend, statrecv, at(z + d, 0)).start())

        def share(zz, src, b):
            for k in range(1, TEAM):
                remote(src, acts.at[q, zz], partsend, partrecv.at[b],
                       {"groups": group_at((q + k) % TEAM)}).start()

        def hand_over(p, zz, src):
            remote(src, acts.at[p, zz], northsend, northrecv, sibling).start()

        send_rows(0)
        share(z, for_chip(z), 0)
        hand_over(q, z, for_chip(z))

        count = float(2 * wide * GROUP)
        first = pack(jnp.sum(flat[...].reshape(wide, 8, LANES), axis=0), 0)
        mean = unpack(first, 0) * (1.0 / count)
        second = pack(jnp.sum((flat[...].reshape(wide, 8, LANES) - mean[None]) ** 2, axis=0), 1)
        row[...] = first + second
        stats[z] = row[...]
        acts[q, z] = cells[pl.ds(z * 4, 6)]
        send_stats(0)

        for k in range(len(rounds)):
            pl.semaphore_wait(ask.at[k], 2)
            tell(k + 1)
            send_rows(k + 1)
            send_stats(k + 1)

        for b in range(len(spans)):
            wait_bytes(acts.at[0, pl.ds(0, sizes[b])], a2arecv.at[b])

            def body(d):
                zz = lax.rem(z + d + nz, nz)
                share(zz, acts.at[q, zz], b)
                hand_over(q, zz, acts.at[q, zz])
            each(b, body)

        wait_bytes(stats.at[pl.ds(0, nz - 1)], statrecv)
        every = stats[...].reshape(nz, LANES)
        lane = lax.broadcasted_iota(jnp.int32, (nz, LANES), 1)
        mean = jnp.sum(every, axis=0, keepdims=True) * (1.0 / (count * nz))
        off = jnp.where(lane < 32, (every * (1.0 / count) - mean) ** 2 * count, 0.0)
        spread = jnp.where(lane < 32, 0.0, every)
        spread = jnp.sum(spread + pltpu.roll(off, 32, 1), axis=0, keepdims=True) * (1.0 / (count * nz))
        tot[...] = jnp.where(lane[:1] < 32, mean, spread)
        totals[q] = tot[...]
        for k in range(1, TEAM):
            remote(tot, totals.at[q], totsend.at[0], totrecv.at[0],
                   {"groups": group_at((q + k) % TEAM)}).start()
        wait_bytes(totals.at[pl.ds(0, TEAM - 1)], totrecv.at[0])
        remote(totals, totals, totsend.at[1], totrecv.at[1], sibling).start()

        for b in range(len(spans)):
            n = sizes[b] + (1 if b == 0 else 0)
            wait_bytes(acts.at[pl.ds(0, TEAM - 1), pl.ds(0, n)], partrecv.at[b])

            def body(d):
                zz = lax.rem(z + d + nz, nz)
                for k in range(1, TEAM):
                    p = lax.rem(q + k, TEAM)
                    hand_over(p, zz, acts.at[p, zz])
            if b == 0:
                body(0)
            each(b, body)

        wait_bytes(w.at[:, 0], giverecv.at[half])
        blend(z)

        @pl.loop(0, half - 1)
        def _(s):
            wait_bytes(w.at[:, pl.ds(0, 4)], giverecv.at[s])
            blend(z - s - 1)
            blend(z + s + 1)

        wait_bytes(w.at[:, pl.ds(0, 2)], giverecv.at[half - 1])
        blend(z + half)
        for p in pieces:
            p.wait_send()
        wait_bytes(stats.at[pl.ds(0, nz - 1)], statsend)
        wait_bytes(acts.at[0, pl.ds(0, nz - 1)], a2asend)
        wait_bytes(acts.at[pl.ds(0, TEAM - 1)], partsend)
        wait_bytes(acts, northsend)
        wait_bytes(totals.at[pl.ds(0, TEAM - 1)], totsend.at[0])
        wait_bytes(totals, totsend.at[1])

    channels = a.shape[-1]
    tiles = channels // LANES
    pairs = ROWS // 2
    g = jnp.concatenate([gain[t] for t in range(tiles)] * 2, axis=0)
    b = jnp.concatenate([shift[t] for t in range(tiles)] * 2, axis=0)
    for p in range(TEAM):
        mean = unpack(totals[p], 0)
        scale = g * lax.rsqrt(unpack(totals[p], 1) + EPSILON)
        move = b - mean * scale

        @pl.loop(0, pairs)
        def _(rp):
            for f in range(FRAMES):
                v = acts[p, f * pairs + rp, pl.ds(2 * c, 4)].astype(F32)
                v = v * scale[None] + move[None]
                v = v / (1.0 + jnp.exp(-v))
                start = rp * (16 * YROWS) + (p * FRAMES + f) * YROWS
                ys[pl.ds(pl.multiple_of(start, 8), 32)] = v.reshape(32, LANES)

    @pl.loop(0, pairs)
    def _(rp):
        for col in range(4):
            for r in range(2):
                for t in range(tiles):
                    v = ys[pl.ds(rp * (16 * YROWS) + col * 8 + r * tiles + t, 16, stride=YROWS)].astype(BF16)
                    a[rp * 2 + r + 1, col, :, t * LANES:(t + 1) * LANES] = v

    a[0] = a[1]
    a[ROWS + 1] = a[ROWS]

    frame = lax.broadcasted_iota(jnp.int32, (8, LANES), 0) % FRAMES
    few = ROWS // 2
    for h in range(2):
        for dt in (2, 1, 0):
            dst = total if dt == 2 else acc
            col0 = 0
            for dr, dc in SHIFTS:
                ps = phases_of(dr, dc)
                lhs = a[1 + dr + h * few:1 + dr + (h + 1) * few, 1 + dc:3 + dc].reshape(few * 2 * 16, channels)
                r = jnp.dot(lhs, mix[dt, :, col0:col0 + len(ps) * LANES], preferred_element_type=F32)
                col0 += len(ps) * LANES
                if (dr, dc) == (0, 0):
                    dst[...] = r
                else:
                    for n, (pr, pc) in enumerate(ps):
                        cols = slice((pr * 2 + pc) * LANES, (pr * 2 + pc + 1) * LANES)
                        dst[:, cols] += r[:, n * LANES:(n + 1) * LANES]
            if dt != 2:
                @pl.loop(0, acc.shape[0] // 8)
                def _(i):
                    rows = pl.ds(pl.multiple_of(i * 8, 8), 8)
                    for n in range(4):
                        cols = slice(n * LANES, (n + 1) * LANES)
                        v = acc[rows, cols]
                        moved = jnp.where(frame >= 1, pltpu.roll(v, 1, 0), v)
                        if dt == 0:
                            moved = jnp.where(frame >= 2, pltpu.roll(v, 2, 0), moved)
                        total[rows, cols] += moved

        bias_row = bias[q].astype(F32)
        for r in range(few):
            for cc in range(2):
                for n in range(4):
                    pr, pc = n // 2, n % 2
                    i = ((r * 2 + pr) * 2 + cc) * 2 + pc
                    turn[i * TROWS:i * TROWS + 16] = total[(r * 2 + cc) * 16:(r * 2 + cc + 1) * 16, n * LANES:(n + 1) * LANES] + bias_row
        put = slice(h * ROWS, (h + 1) * ROWS)
        for p in range(TEAM):
            for f in range(FRAMES):
                v = turn[pl.ds(p * FRAMES + f, few * 8, stride=TROWS)].astype(BF16)
                mine[p, f, put] = v.reshape(ROWS, 4, LANES)
        here = pl.ds(pl.multiple_of(q * LANES, LANES), LANES)
        for k in (3, 2, 1):
            p = lax.rem(q + k, TEAM)
            remote(mine.at[p, :, put], out.at[:, put, :, here], outsend, outrecv, {"groups": group_at(p)}).start()
        out[:, put, :, here] = mine[q, :, put]
    wait_bytes(mine.at[pl.ds(0, TEAM - 1)], outrecv)
    wait_bytes(mine.at[pl.ds(0, TEAM - 1)], outsend)


VMEM = pl.BlockSpec(memory_space=pltpu.VMEM)
ANY = pl.BlockSpec(memory_space=pl.ANY)


def shards(ny, hidden, norm_gain, norm_shift, conv_weight, conv_bias):
    nd = lax.axis_size("space")
    nz = nd // 2
    wide, channels = hidden.shape
    tiles = channels // LANES
    cin = conv_weight.shape[3]
    batches = len(rounds_of(nz // 2)) + 1
    wq = conv_weight.reshape(3, TAPS, cin, conv_weight.shape[4])
    scratch = [
        pltpu.VMEM((3, nd, TAPS, cin, LANES), BF16),
        pltpu.VMEM((3, channels, 16 * LANES), BF16),
        pltpu.VMEM((TEAM, nz, 6, 8, LANES), BF16),
        pltpu.VMEM((TEAM, 1, LANES), F32),
        pltpu.VMEM((2, wide, channels), BF16),
        pltpu.VMEM((wide + 2, 8, LANES), BF16),
        pltpu.VMEM((wide * 8, LANES), F32),
        pltpu.VMEM((nz, 1, LANES), F32),
        pltpu.VMEM((1, LANES), F32),
        pltpu.VMEM((1, LANES), F32),
        pltpu.VMEM((ROWS // 2 * 16 * YROWS, LANES), F32),
        pltpu.VMEM((ROWS + 2, 4, 16, channels), BF16),
        pltpu.VMEM((ROWS * 16, 4 * LANES), F32),
        pltpu.VMEM((ROWS * 16, 4 * LANES), F32),
        pltpu.VMEM((ROWS * 4 * TROWS, LANES), F32),
        pltpu.VMEM((TEAM, FRAMES, ROWS * 2, 4, LANES), BF16),
        DMA((2,)), DMA((2,)), DMA((2, nz // 2, 3)), DMA, DMA((nz // 2 + 1,)), DMA((2, 4)),
        pltpu.SemaphoreType.REGULAR((max(1, batches - 1),)),
        DMA, DMA((batches,)), DMA, DMA, DMA, DMA((batches,)), DMA, DMA, DMA((2,)), DMA((2,)), DMA, DMA,
    ]
    return pl.pallas_call(
        functools.partial(kernel, ny, nd),
        out_shape=jax.ShapeDtypeStruct((FRAMES, ROWS * 2, 4, channels), BF16),
        in_specs=[ANY, ANY, VMEM, VMEM, VMEM],
        out_specs=VMEM,
        scratch_shapes=scratch,
        compiler_params=pltpu.CompilerParams(collective_id=0, has_side_effects=True, vmem_limit_bytes=56 * MIB),
        name="decode",
    )(hidden, wq, norm_gain.reshape(tiles, 1, LANES), norm_shift.reshape(tiles, 1, LANES), conv_bias.reshape(tiles, 1, LANES))


def solution(mesh):
    ny = len({d.coords[1] for d in mesh.devices.flat})
    return jax.shard_map(
        functools.partial(shards, ny),
        mesh=mesh,
        in_specs=(P(("groups", "space"), None), P(), P(), P(None, None, None, "space", None), P()),
        out_specs=P("groups", None, "space", None),
        check_vma=False,
    )
```

time: 113 us -> 99.9 us (0.88)
  Pallas kernels: 105 us -> 96.4 us
  local copies, waits for them, and re-layouts: 6.26 us -> 3.27 us
    pallas_call x3 -> x1, Pallas kernels: 105 us -> 96.4 us  [shards(): pl.pallas_call(functools.partial(kernel, ny, nd), out_shape=jax.ShapeDtyp...]
    reshape x3 -> x1, local copies, waits for them, and re-layouts: 3.08 us -> 0.58 us  [shards(): conv_bias.reshape(tiles, 1, LANES)]
    unnamed x8 -> x3, local copies, waits for them, and re-layouts: 3.08 us -> 2.69 us
where the time goes in v2:
time: 99.9 us; the launch traced here: 99.7 us
  Pallas kernels  96.4 us (96%)
  local copies, waits for them, and re-layouts  3.27 us (3%)
    pallas_call x1, Pallas kernels, shards(): pl.pallas_call(functools.partial(kernel, ny, nd), out_shape=jax.ShapeDtyp...  96.4 us
    unnamed x3, local copies, waits for them, and re-layouts  2.69 us

profile of v2, /device:TPU:37, one launch (start us, length us, event | category | flops | bytes accessed | tf_op | source)
XLA Modules:
  0.0 99.7 jit_solution(10384594492978080209)
XLA Ops:
  0.0 0.0 copy-start
  0.0 0.7 copy-done
  0.7 0.6 copy.6.bias
  1.3 96.4 %decode.1 = bf16[4,32,4,512]{3,2,1,0:T(4,128)(2,1)} custom-call(bf16[128,512]{1,0:T(8,128)(2,1)} %h_ref.1, bf16[3,9,8,512]{3,2,1,0:T(8,128)(2,1)} %bitcast.4, f32[4,1,128]{2,1,0:T(1,128)} %bitcast.5, f32[4,1,128]{2,1,0:T(1,128)} %bitcast.6, bf16[4,1,128]{2,1,0:T(2,128)(2,1)} %copy.6.bias), custom_call_target="tpu_custom_call" | custom-call | tf_op jit(solution)/shard_map/decode/pallas_call | solution.py:452
  97.7 2.0 %copy.8 = bf16[4,32,4,512]{3,2,1,0:T(4,128)(2,1)} copy(bf16[4,32,4,512]{3,2,1,0:T(4,128)(2,1)} %decode.1) | data formatting | bytes 1048576
Async XLA Ops:
  0.0 0.7 copy-start

commit v3 on v2

--- a/solution.py
+++ b/solution.py
@@ -17,6 +17,7 @@
 MIB = 1 << 20
 YROWS = 40
 TROWS = 24
+NEAR = 5
 
 DMA = pltpu.SemaphoreType.DMA
 F32, BF16 = jnp.float32, jnp.bfloat16
@@ -87,15 +88,17 @@
     return steps
 
 
-def kernel(ny, nd, h_ref, wq_ref, gain, shift, bias, out,
+def kernel(ny, nd, h_ref, wq_ref, gain_ref, shift_ref, bias_ref, out, gain, shift, bias,
            w, mix, acts, totals, raw, cells, flat, stats, row, tot, ys, a, acc, total, turn, mine,
            local, ringsend, ringrecv, give, giverecv, own, ask, a2asend, a2arecv,
-           statsend, statrecv, partsend, partrecv, northsend, northrecv, totsend, totrecv, outsend, outrecv):
+           statsend, statrecv, partsend, partrecv, northsend, northrecv, edgesend, edgerecv, totsend, totrecv, outsend, outrecv):
     me = lax.axis_index("space")
     z, c = me // 2, me % 2
     nz = nd // 2
     half = nz // 2
     q, group_at = team(ny)
+    leaps = (half - NEAR + 1) // 2
+    assert NEAR + 2 * leaps == half + 1
     rounds = rounds_of(half)
     spans, last = [], 0
     for known in [1] + [r[1] for r in rounds]:
@@ -122,8 +125,45 @@
             for n, ((dr, dc), (pr, pc)) in enumerate(COLUMNS):
                 mix[dt, pl.ds(pl.multiple_of(zz * 16, 16), 16), n * LANES:(n + 1) * LANES] = both[(pr, dr)][(pc, dc)].astype(BF16)
 
+    channels = a.shape[-1]
+    tiles = channels // LANES
+    pairs = ROWS // 2
+
+    def activate():
+        for copy in small:
+            copy.wait()
+        g = jnp.concatenate([gain[t] for t in range(tiles)] * 2, axis=0)
+        b = jnp.concatenate([shift[t] for t in range(tiles)] * 2, axis=0)
+        for p in range(TEAM):
+            mean = unpack(totals[p], 0)
+            scale = g * lax.rsqrt(unpack(totals[p], 1) + EPSILON)
+            move = (b - mean * scale) * 0.5
+            scale = scale * 0.5
+
+            @pl.loop(0, pairs, unroll=4)
+            def _(rp):
+                for f in range(FRAMES):
+                    v = acts[p, f * pairs + rp, pl.ds(2 * c, 4)].astype(F32)
+                    v = v * scale[None] + move[None]
+                    v = v * jnp.tanh(v) + v
+                    start = rp * (16 * YROWS) + (p * FRAMES + f) * YROWS
+                    ys[pl.ds(pl.multiple_of(start, 8), 32)] = v.reshape(32, LANES)
+
+        @pl.loop(0, pairs)
+        def _(rp):
+            for col in range(4):
+                for r in range(2):
+                    for t in range(tiles):
+                        v = ys[pl.ds(rp * (16 * YROWS) + col * 8 + r * tiles + t, 16, stride=YROWS)].astype(BF16)
+                        a[rp * 2 + r + 1, col, :, t * LANES:(t + 1) * LANES] = v
+
+        a[0] = a[1]
+        a[ROWS + 1] = a[ROWS]
+
     load = pltpu.make_async_copy(wq_ref.at[:, :, :, pl.ds(q * LANES, LANES)], w.at[:, me], local.at[0])
     rows_in = pltpu.make_async_copy(h_ref, raw.at[0], local.at[1])
+    small = [pltpu.make_async_copy(src, dst, local.at[2 + i])
+             for i, (src, dst) in enumerate(((gain_ref, gain), (shift_ref, shift), (bias_ref, bias)))]
 
     @pl.when(c == 1)
     def _():
@@ -132,6 +172,8 @@
         signal(barrier, sibling)
         load.start()
         rows_in.start()
+        for copy in small:
+            copy.start()
         pl.semaphore_wait(barrier, 3)
         rows_in.wait()
         rows_out = remote(raw.at[0], raw.at[1], own.at[0, 0], own.at[1, 0], sibling)
@@ -141,57 +183,83 @@
         def piece(zz, j):
             return w.at[j, pl.ds(lax.rem(zz + 2 * nz, nz) * 2, 2)]
 
-        def right(p, s, j):
-            return remote(p, p, ringsend.at[0], ringrecv.at[0, s, j], at(z + 1, 1))
-
-        def left(p, s, j):
-            return remote(p, p, ringsend.at[1], ringrecv.at[1, s, j], at(z - 1, 1))
+        def hop(way, p, d, j, step=1):
+            to = z + step if way == 0 else z - step
+            return remote(p, p, ringsend.at[way], ringrecv.at[way, d - 1, j], at(to, 1))
 
         for j in range(3):
             theirs = w.at[j, z * 2]
             remote(theirs, theirs, own.at[0, 1 + j], own.at[1, 1 + j], sibling).wait_recv()
             p = piece(z, j)
-            right(p, 0, j).start()
-            left(p, 0, j).start()
+            for way in (0, 1):
+                hop(way, p, 1, j).start()
             m = w.at[j, me]
             remote(m, m, give, giverecv.at[half], sibling).start()
         blend(z)
 
-        @pl.loop(0, half)
+        def take(way, d, j, s, on):
+            p = piece(z - d if way == 0 else z + d, j)
+            hop(way, p, d, j).wait_recv()
+            for step in on:
+                hop(way, p, d + step, j, step).start()
+            remote(p, p, give, giverecv.at[s], sibling).start()
+
+        @pl.loop(0, NEAR - 1)
         def _(s):
             for j in range(3):
-                p = piece(z - s - 1, j)
-                right(p, s, j).wait_recv()
-
-                @pl.when(s < half - 1)
-                def _():
-                    right(p, s + 1, j).start()
-
-                remote(p, p, give, giverecv.at[s], sibling).start()
-
-                @pl.when(s < half - 1)
-                def _():
-                    o = piece(z + s + 1, j)
-                    left(o, s, j).wait_recv()
-
-                    @pl.when(s < half - 2)
-                    def _():
-                        left(o, s + 1, j).start()
-
-                    remote(o, o, give, giverecv.at[s], sibling).start()
-
+                take(0, s + 1, j, s, (1,))
+                take(1, s + 1, j, s, (1,))
             blend(z - s - 1)
-
-            @pl.when(s < half - 1)
+            blend(z + s + 1)
+
+        @pl.loop(0, leaps - 1)
+        def _(u):
+            d, s = NEAR + 2 * u, NEAR - 1 + u
+            for j in range(3):
+                take(0, d, j, s, (2, 1))
+                take(1, d, j, s, (2, 1))
+            blend(z - d)
+            blend(z + d)
+
+            @pl.when(u > 0)
             def _():
-                blend(z + s + 1)
+                for j in range(3):
+                    take(0, d - 1, j, s, ())
+                    take(1, d - 1, j, s, ())
+                blend(z - d + 1)
+                blend(z + d - 1)
+
+        d, s = half - 1, NEAR - 2 + leaps
+        for j in range(3):
+            take(0, d, j, s, (1,))
+            take(1, d, j, s, ())
+        blend(z - d)
+        blend(z + d)
+        for j in range(3):
+            take(0, d - 1, j, s, ())
+            take(1, d - 1, j, s, ())
+        blend(z - d + 1)
+        blend(z + d - 1)
+        wait_bytes(acts.at[:, :, pl.ds(2, 3)], northrecv)
+        remote(totals, totals, totsend.at[1], totrecv.at[1], sibling).wait_recv()
+
+        @pl.when(z < nz - 1)
+        def _():
+            wait_bytes(acts.at[:, :, 5], edgerecv)
+
+        @pl.when(z == nz - 1)
+        def _():
+            acts[:, :, 5] = acts[:, :, 4]
+
+        activate()
+        for j in range(3):
+            take(0, half, j, s, ())
+        blend(z + half)
 
         rows_out.wait_send()
         wait_bytes(w.at[:, pl.ds(0, 2 * half)], ringsend.at[0])
         wait_bytes(w.at[:, pl.ds(0, 2 * half - 2)], ringsend.at[1])
         wait_bytes(w.at[:, pl.ds(0, nd - 1)], give)
-        wait_bytes(acts, northrecv)
-        remote(totals, totals, totsend.at[1], totrecv.at[1], sibling).wait_recv()
 
     @pl.when(c == 0)
     def _():
@@ -202,6 +270,8 @@
             signal(barrier, {"groups": group_at((q + k) % TEAM)})
         load.start()
         rows_in.start()
+        for copy in small:
+            copy.start()
         pl.semaphore_wait(barrier, 2 + TEAM)
 
         def tell(k):
@@ -216,18 +286,19 @@
             p = w.at[j, me]
             pieces.append(remote(p, p, own.at[0, 1 + j], own.at[1, 1 + j], sibling))
             pieces[-1].start()
+        early = min(2, len(rounds))
+        for k in range(early):
+            pl.semaphore_wait(ask.at[k], 2)
+            tell(k + 1)
         rows_in.wait()
         remote(raw.at[0], raw.at[1], own.at[0, 0], own.at[1, 0], sibling).wait_recv()
 
         wide = raw.shape[1]
-        tiles = raw.shape[2] // LANES
         for r in range(2):
             for t in range(tiles):
                 flat[pl.ds(r * tiles + t, wide, stride=8)] = raw[r, :, t * LANES:(t + 1) * LANES].astype(F32)
         x = flat[...].reshape(wide, 8, LANES)
-        cells[pl.ds(1, wide)] = x.astype(BF16)
-        cells[0] = x[0].astype(BF16)
-        cells[wide + 1] = x[wide - 1].astype(BF16)
+        cells[...] = x.astype(BF16)
 
         def each(b, body):
             lo, hi = spans[b]
@@ -240,13 +311,16 @@
             if hi == half:
                 body(half)
 
+        middle = pl.ds(1, 4)
+        norths = pl.ds(2, 3)
+
         def for_chip(zz):
-            return cells.at[pl.ds(zz * 4, 6)]
+            return cells.at[pl.ds(zz * 4, 4)]
 
         def send_rows(b):
             def body(d):
                 zz = lax.rem(z + d + nz, nz)
-                remote(for_chip(zz), acts.at[q, z], a2asend, a2arecv.at[b], at(zz, 0)).start()
+                remote(for_chip(zz), acts.at[q, z, middle], a2asend, a2arecv.at[b], at(zz, 0)).start()
             each(b, body)
 
         def send_stats(b):
@@ -254,15 +328,16 @@
 
         def share(zz, src, b):
             for k in range(1, TEAM):
-                remote(src, acts.at[q, zz], partsend, partrecv.at[b],
+                remote(src, acts.at[q, zz, middle], partsend, partrecv.at[b],
                        {"groups": group_at((q + k) % TEAM)}).start()
 
         def hand_over(p, zz, src):
-            remote(src, acts.at[p, zz], northsend, northrecv, sibling).start()
-
-        send_rows(0)
+            remote(src, acts.at[p, zz, norths], northsend, northrecv, sibling).start()
+
+        for b in range(early + 1):
+            send_rows(b)
         share(z, for_chip(z), 0)
-        hand_over(q, z, for_chip(z))
+        hand_over(q, z, cells.at[pl.ds(z * 4 + 1, 3)])
 
         count = float(2 * wide * GROUP)
         first = pack(jnp.sum(flat[...].reshape(wide, 8, LANES), axis=0), 0)
@@ -270,23 +345,51 @@
         second = pack(jnp.sum((flat[...].reshape(wide, 8, LANES) - mean[None]) ** 2, axis=0), 1)
         row[...] = first + second
         stats[z] = row[...]
-        acts[q, z] = cells[pl.ds(z * 4, 6)]
-        send_stats(0)
-
-        for k in range(len(rounds)):
+        acts[q, z, 1:5] = cells[pl.ds(z * 4, 4)]
+        for b in range(early + 1):
+            send_stats(b)
+
+        for k in range(early, len(rounds)):
             pl.semaphore_wait(ask.at[k], 2)
             tell(k + 1)
             send_rows(k + 1)
             send_stats(k + 1)
 
         for b in range(len(spans)):
-            wait_bytes(acts.at[0, pl.ds(0, sizes[b])], a2arecv.at[b])
+            wait_bytes(acts.at[0, pl.ds(0, sizes[b]), middle], a2arecv.at[b])
 
             def body(d):
                 zz = lax.rem(z + d + nz, nz)
-                share(zz, acts.at[q, zz], b)
-                hand_over(q, zz, acts.at[q, zz])
+                share(zz, acts.at[q, zz, middle], b)
+                hand_over(q, zz, acts.at[q, zz, norths])
             each(b, body)
+
+        def from_team(b):
+            n = sizes[b] + (1 if b == 0 else 0)
+            wait_bytes(acts.at[pl.ds(0, TEAM - 1), pl.ds(0, n), middle], partrecv.at[b])
+
+            def body(d):
+                zz = lax.rem(z + d + nz, nz)
+                for k in range(1, TEAM):
+                    p = lax.rem(q + k, TEAM)
+                    hand_over(p, zz, acts.at[p, zz, norths])
+            if b == 0:
+                body(0)
+            each(b, body)
+
+        from_team(0)
+        for k in range(TEAM):
+            g = group_at((q + k) % TEAM)
+
+            @pl.when(z < nz - 1)
+            def _():
+                remote(acts.at[q, :, 4], acts.at[q, :, 0], edgesend.at[0], edgerecv,
+                       {"groups": g, "space": z * 2 + 2}).start()
+
+            @pl.when(z > 0)
+            def _():
+                remote(acts.at[q, :, 1], acts.at[q, :, 5], edgesend.at[1], edgerecv,
+                       {"groups": g, "space": z * 2 - 1}).start()
 
         wait_bytes(stats.at[pl.ds(0, nz - 1)], statrecv)
         every = stats[...].reshape(nz, LANES)
@@ -303,68 +406,59 @@
         wait_bytes(totals.at[pl.ds(0, TEAM - 1)], totrecv.at[0])
         remote(totals, totals, totsend.at[1], totrecv.at[1], sibling).start()
 
-        for b in range(len(spans)):
-            n = sizes[b] + (1 if b == 0 else 0)
-            wait_bytes(acts.at[pl.ds(0, TEAM - 1), pl.ds(0, n)], partrecv.at[b])
-
-            def body(d):
-                zz = lax.rem(z + d + nz, nz)
-                for k in range(1, TEAM):
-                    p = lax.rem(q + k, TEAM)
-                    hand_over(p, zz, acts.at[p, zz])
-            if b == 0:
-                body(0)
-            each(b, body)
-
+        for b in range(1, len(spans)):
+            from_team(b)
+
+        @pl.when(z > 0)
+        def _():
+            wait_bytes(acts.at[:, :, 0], edgerecv)
+
+        @pl.when(z == 0)
+        def _():
+            acts[:, :, 0] = acts[:, :, 1]
+
+        activate()
         wait_bytes(w.at[:, 0], giverecv.at[half])
         blend(z)
 
-        @pl.loop(0, half - 1)
+        @pl.loop(0, NEAR - 1)
         def _(s):
             wait_bytes(w.at[:, pl.ds(0, 4)], giverecv.at[s])
             blend(z - s - 1)
             blend(z + s + 1)
 
-        wait_bytes(w.at[:, pl.ds(0, 2)], giverecv.at[half - 1])
+        wait_bytes(w.at[:, pl.ds(0, 4)], giverecv.at[NEAR - 1])
+        blend(z - NEAR)
+        blend(z + NEAR)
+
+        @pl.loop(1, leaps - 1)
+        def _(u):
+            wait_bytes(w.at[:, pl.ds(0, 8)], giverecv.at[NEAR - 1 + u])
+            for d in (0, -1):
+                blend(z - NEAR - 2 * u - d)
+                blend(z + NEAR + 2 * u + d)
+
+        wait_bytes(w.at[:, pl.ds(0, 10)], giverecv.at[NEAR - 2 + leaps])
+        for d in (half - 2, half - 1):
+            blend(z - d)
+            blend(z + d)
         blend(z + half)
         for p in pieces:
             p.wait_send()
         wait_bytes(stats.at[pl.ds(0, nz - 1)], statsend)
-        wait_bytes(acts.at[0, pl.ds(0, nz - 1)], a2asend)
-        wait_bytes(acts.at[pl.ds(0, TEAM - 1)], partsend)
-        wait_bytes(acts, northsend)
+        wait_bytes(acts.at[0, pl.ds(0, nz - 1), middle], a2asend)
+        wait_bytes(acts.at[pl.ds(0, TEAM - 1), :, middle], partsend)
+        wait_bytes(acts.at[:, :, norths], northsend)
+
+        @pl.when(z < nz - 1)
+        def _():
+            wait_bytes(acts.at[:, :, 0], edgesend.at[0])
+
+        @pl.when(z > 0)
+        def _():
+            wait_bytes(acts.at[:, :, 0], edgesend.at[1])
         wait_bytes(totals.at[pl.ds(0, TEAM - 1)], totsend.at[0])
         wait_bytes(totals, totsend.at[1])
-
-    channels = a.shape[-1]
-    tiles = channels // LANES
-    pairs = ROWS // 2
-    g = jnp.concatenate([gain[t] for t in range(tiles)] * 2, axis=0)
-    b = jnp.concatenate([shift[t] for t in range(tiles)] * 2, axis=0)
-    for p in range(TEAM):
-        mean = unpack(totals[p], 0)
-        scale = g * lax.rsqrt(unpack(totals[p], 1) + EPSILON)
-        move = b - mean * scale
-
-        @pl.loop(0, pairs)
-        def _(rp):
-            for f in range(FRAMES):
-                v = acts[p, f * pairs + rp, pl.ds(2 * c, 4)].astype(F32)
-                v = v * scale[None] + move[None]
-                v = v / (1.0 + jnp.exp(-v))
-                start = rp * (16 * YROWS) + (p * FRAMES + f) * YROWS
-                ys[pl.ds(pl.multiple_of(start, 8), 32)] = v.reshape(32, LANES)
-
-    @pl.loop(0, pairs)
-    def _(rp):
-        for col in range(4):
-            for r in range(2):
-                for t in range(tiles):
-                    v = ys[pl.ds(rp * (16 * YROWS) + col * 8 + r * tiles + t, 16, stride=YROWS)].astype(BF16)
-                    a[rp * 2 + r + 1, col, :, t * LANES:(t + 1) * LANES] = v
-
-    a[0] = a[1]
-    a[ROWS + 1] = a[ROWS]
 
     frame = lax.broadcasted_iota(jnp.int32, (8, LANES), 0) % FRAMES
     few = ROWS // 2
@@ -395,7 +489,7 @@
                             moved = jnp.where(frame >= 2, pltpu.roll(v, 2, 0), moved)
                         total[rows, cols] += moved
 
-        bias_row = bias[q].astype(F32)
+        bias_row = bias[q]
         for r in range(few):
             for cc in range(2):
                 for n in range(4):
@@ -417,7 +511,7 @@
 
 
 VMEM = pl.BlockSpec(memory_space=pltpu.VMEM)
-ANY = pl.BlockSpec(memory_space=pl.ANY)
+HBM = pl.BlockSpec(memory_space=pltpu.HBM)
 
 
 def shards(ny, hidden, norm_gain, norm_shift, conv_weight, conv_bias):
@@ -428,13 +522,13 @@
     cin = conv_weight.shape[3]
     batches = len(rounds_of(nz // 2)) + 1
     wq = conv_weight.reshape(3, TAPS, cin, conv_weight.shape[4])
-    scratch = [
+    scratch = [pltpu.VMEM((tiles, 1, LANES), F32)] * 3 + [
         pltpu.VMEM((3, nd, TAPS, cin, LANES), BF16),
         pltpu.VMEM((3, channels, 16 * LANES), BF16),
         pltpu.VMEM((TEAM, nz, 6, 8, LANES), BF16),
         pltpu.VMEM((TEAM, 1, LANES), F32),
         pltpu.VMEM((2, wide, channels), BF16),
-        pltpu.VMEM((wide + 2, 8, LANES), BF16),
+        pltpu.VMEM((wide, 8, LANES), BF16),
         pltpu.VMEM((wide * 8, LANES), F32),
         pltpu.VMEM((nz, 1, LANES), F32),
         pltpu.VMEM((1, LANES), F32),
@@ -445,19 +539,19 @@
         pltpu.VMEM((ROWS * 16, 4 * LANES), F32),
         pltpu.VMEM((ROWS * 4 * TROWS, LANES), F32),
         pltpu.VMEM((TEAM, FRAMES, ROWS * 2, 4, LANES), BF16),
-        DMA((2,)), DMA((2,)), DMA((2, nz // 2, 3)), DMA, DMA((nz // 2 + 1,)), DMA((2, 4)),
+        DMA((5,)), DMA((2,)), DMA((2, nz // 2, 3)), DMA, DMA((nz // 2 + 1,)), DMA((2, 4)),
         pltpu.SemaphoreType.REGULAR((max(1, batches - 1),)),
-        DMA, DMA((batches,)), DMA, DMA, DMA, DMA((batches,)), DMA, DMA, DMA((2,)), DMA((2,)), DMA, DMA,
+        DMA, DMA((batches,)), DMA, DMA, DMA, DMA((batches,)), DMA, DMA, DMA((2,)), DMA, DMA((2,)), DMA((2,)), DMA, DMA,
     ]
     return pl.pallas_call(
         functools.partial(kernel, ny, nd),
         out_shape=jax.ShapeDtypeStruct((FRAMES, ROWS * 2, 4, channels), BF16),
-        in_specs=[ANY, ANY, VMEM, VMEM, VMEM],
+        in_specs=[HBM] * 5,
         out_specs=VMEM,
         scratch_shapes=scratch,
         compiler_params=pltpu.CompilerParams(collective_id=0, has_side_effects=True, vmem_limit_bytes=56 * MIB),
         name="decode",
-    )(hidden, wq, norm_gain.reshape(tiles, 1, LANES), norm_shift.reshape(tiles, 1, LANES), conv_bias.reshape(tiles, 1, LANES))
+    )(hidden, wq, norm_gain.reshape(tiles, 1, LANES), norm_shift.reshape(tiles, 1, LANES), conv_bias.astype(F32).reshape(tiles, 1, LANES))
 
 
 def solution(mesh):

time: 99.9 us -> 88.8 us (0.89)
  Pallas kernels: 96.4 us -> 85.4 us
    pallas_call x1, Pallas kernels: 96.4 us -> 85.4 us  [shards(): pl.pallas_call(functools.partial(kernel, ny, nd), out_shape=jax.ShapeDtyp...]
where the time goes in v3:
time: 88.8 us; the launch traced here: 88.7 us
  Pallas kernels  85.4 us (96%)
  local copies, waits for them, and re-layouts  2.69 us (3%)
    pallas_call x1, Pallas kernels, shards(): pl.pallas_call(functools.partial(kernel, ny, nd), out_shape=jax.ShapeDtyp...  85.4 us
    unnamed x3, local copies, waits for them, and re-layouts  2.69 us

profile of v3, /device:TPU:37, one launch (start us, length us, event | category | flops | bytes accessed | tf_op | source)
XLA Modules:
  0.0 88.7 jit_solution(290689424633769074)
XLA Ops:
  0.0 0.0 copy-start
  0.0 0.7 copy-done
  0.7 0.6 reshape.19
  1.3 85.4 %decode.1 = bf16[4,32,4,512]{3,2,1,0:T(4,128)(2,1)} custom-call(bf16[128,512]{1,0:T(8,128)(2,1)} %h_ref.1, bf16[3,9,8,512]{3,2,1,0:T(8,128)(2,1)} %bitcast.4, f32[4,1,128]{2,1,0:T(1,128)} %bitcast.6, f32[4,1,128]{2,1,0:T(1,128)} %bitcast.7, f32[4,1,128]{2,1,0:T(1,128)} %bitcast.5), custom_call_target="tpu_custom_call" | custom-call | tf_op jit(solution)/shard_map/decode/pallas_call | solution.py:546
  86.6 2.0 %copy.7 = bf16[4,32,4,512]{3,2,1,0:T(4,128)(2,1)} copy(bf16[4,32,4,512]{3,2,1,0:T(4,128)(2,1)} %decode.1) | data formatting | bytes 1048576
Async XLA Ops:
  0.0 0.7 copy-start

commit v4 on v3

--- a/solution.py
+++ b/solution.py
@@ -17,7 +17,7 @@
 MIB = 1 << 20
 YROWS = 40
 TROWS = 24
-NEAR = 5
+NEAR = 6
 
 DMA = pltpu.SemaphoreType.DMA
 F32, BF16 = jnp.float32, jnp.bfloat16
@@ -89,7 +89,7 @@
 
 
 def kernel(ny, nd, h_ref, wq_ref, gain_ref, shift_ref, bias_ref, out, gain, shift, bias,
-           w, mix, acts, totals, raw, cells, flat, stats, row, tot, ys, a, acc, total, turn, mine,
+           w, mix, acts, totals, raw, cells, flat, stats, row, tot, ys, a, acc, turn, mine,
            local, ringsend, ringrecv, give, giverecv, own, ask, a2asend, a2arecv,
            statsend, statrecv, partsend, partrecv, northsend, northrecv, edgesend, edgerecv, totsend, totrecv, outsend, outrecv):
     me = lax.axis_index("space")
@@ -97,8 +97,8 @@
     nz = nd // 2
     half = nz // 2
     q, group_at = team(ny)
-    leaps = (half - NEAR + 1) // 2
-    assert NEAR + 2 * leaps == half + 1
+    leaps = (half - NEAR) // 2
+    assert NEAR + 2 * leaps == half
     rounds = rounds_of(half)
     spans, last = [], 0
     for known in [1] + [r[1] for r in rounds]:
@@ -115,7 +115,7 @@
     def blend(zz):
         zz = lax.rem(zz + 2 * nz, nz)
         for dt in range(3):
-            tap = [w[dt, pl.ds(zz * 2, 2), n].reshape(16, LANES).astype(F32) for n in range(TAPS)]
+            tap = [w[dt, pl.ds(zz * 2, 2), n].astype(F32).reshape(16, LANES) for n in range(TAPS)]
 
             def sums(x):
                 return {(0, -1): x[0], (0, 0): x[1] + x[2], (1, 0): x[0] + x[1], (1, 1): x[2]}
@@ -129,12 +129,10 @@
     tiles = channels // LANES
     pairs = ROWS // 2
 
-    def activate():
-        for copy in small:
-            copy.wait()
+    def activate(places):
         g = jnp.concatenate([gain[t] for t in range(tiles)] * 2, axis=0)
         b = jnp.concatenate([shift[t] for t in range(tiles)] * 2, axis=0)
-        for p in range(TEAM):
+        for p in places:
             mean = unpack(totals[p], 0)
             scale = g * lax.rsqrt(unpack(totals[p], 1) + EPSILON)
             move = (b - mean * scale) * 0.5
@@ -149,6 +147,7 @@
                     start = rp * (16 * YROWS) + (p * FRAMES + f) * YROWS
                     ys[pl.ds(pl.multiple_of(start, 8), 32)] = v.reshape(32, LANES)
 
+    def arrange():
         @pl.loop(0, pairs)
         def _(rp):
             for col in range(4):
@@ -159,6 +158,29 @@
 
         a[0] = a[1]
         a[ROWS + 1] = a[ROWS]
+
+    few = ROWS // 2
+    chips = LANES // 16
+    first_block = z // chips + jnp.where(z % chips < chips // 2, tiles - 1, 0)
+    assert half - 4 >= chips * 3 // 2 - 1 and tiles == 4
+
+    def multiply(h, late):
+        blocks = [pl.ds(pl.multiple_of(lax.rem(first_block + 2 * late + i, tiles) * LANES, LANES), LANES) for i in range(2)]
+        for dt in range(3):
+            col0 = 0
+            for dr, dc in SHIFTS:
+                ps = phases_of(dr, dc)
+                rows, cols = slice(1 + dr + h * few, 1 + dr + (h + 1) * few), slice(1 + dc, 3 + dc)
+                lhs = jnp.concatenate([a[rows, cols, :, k].reshape(few * 2 * 16, LANES) for k in blocks], axis=1)
+                rhs = jnp.concatenate([mix[dt, k, col0:col0 + len(ps) * LANES] for k in blocks], axis=0)
+                r = jnp.dot(lhs, rhs, preferred_element_type=F32)
+                col0 += len(ps) * LANES
+                if (dr, dc) == (0, 0):
+                    acc[h, dt] = acc[h, dt] + r if late else r
+                else:
+                    for n, (pr, pc) in enumerate(ps):
+                        to = slice((pr * 2 + pc) * LANES, (pr * 2 + pc + 1) * LANES)
+                        acc[h, dt, :, to] += r[:, n * LANES:(n + 1) * LANES]
 
     load = pltpu.make_async_copy(wq_ref.at[:, :, :, pl.ds(q * LANES, LANES)], w.at[:, me], local.at[0])
     rows_in = pltpu.make_async_copy(h_ref, raw.at[0], local.at[1])
@@ -187,14 +209,18 @@
             to = z + step if way == 0 else z - step
             return remote(p, p, ringsend.at[way], ringrecv.at[way, d - 1, j], at(to, 1))
 
+        def first(part, j):
+            for way in (0, 1):
+                hop(way, part, 1, j).start()
+
+        for j in range(3):
+            m = w.at[j, me]
+            first(m, j)
+            remote(m, m, give, giverecv.at[half], sibling).start()
         for j in range(3):
             theirs = w.at[j, z * 2]
             remote(theirs, theirs, own.at[0, 1 + j], own.at[1, 1 + j], sibling).wait_recv()
-            p = piece(z, j)
-            for way in (0, 1):
-                hop(way, p, 1, j).start()
-            m = w.at[j, me]
-            remote(m, m, give, giverecv.at[half], sibling).start()
+            first(theirs, j)
         blend(z)
 
         def take(way, d, j, s, on):
@@ -221,6 +247,23 @@
             blend(z - d)
             blend(z + d)
 
+            @pl.when(u == leaps - 2)
+            def _():
+                wait_bytes(acts.at[:, :, pl.ds(2, 3)], northrecv)
+                remote(totals, totals, totsend.at[1], totrecv.at[1], sibling).wait_recv()
+
+                @pl.when(z < nz - 1)
+                def _():
+                    wait_bytes(acts.at[:, :, 5], edgerecv)
+
+                @pl.when(z == nz - 1)
+                def _():
+                    acts[:, :, 5] = acts[:, :, 4]
+
+                for copy in small:
+                    copy.wait()
+                activate((0, 1))
+
             @pl.when(u > 0)
             def _():
                 for j in range(3):
@@ -229,10 +272,12 @@
                 blend(z - d + 1)
                 blend(z + d - 1)
 
-        d, s = half - 1, NEAR - 2 + leaps
+        activate((2, 3))
+        arrange()
+        d, s = half - 2, NEAR - 2 + leaps
         for j in range(3):
-            take(0, d, j, s, (1,))
-            take(1, d, j, s, ())
+            take(0, d, j, s, (2, 1) if j < 2 else (1,))
+            take(1, d, j, s, (1,) if j < 2 else (2, 1))
         blend(z - d)
         blend(z + d)
         for j in range(3):
@@ -240,25 +285,22 @@
             take(1, d - 1, j, s, ())
         blend(z - d + 1)
         blend(z + d - 1)
-        wait_bytes(acts.at[:, :, pl.ds(2, 3)], northrecv)
-        remote(totals, totals, totsend.at[1], totrecv.at[1], sibling).wait_recv()
-
-        @pl.when(z < nz - 1)
-        def _():
-            wait_bytes(acts.at[:, :, 5], edgerecv)
-
-        @pl.when(z == nz - 1)
-        def _():
-            acts[:, :, 5] = acts[:, :, 4]
-
-        activate()
+        multiply(0, 0)
+        multiply(1, 0)
+        s = NEAR - 1 + leaps
         for j in range(3):
-            take(0, half, j, s, ())
+            take(0, half - 1, j, s, ())
+            take(1, half - 1, j, s, ())
+        blend(z - half + 1)
+        blend(z + half - 1)
+        for j in range(3):
+            take(0 if j < 2 else 1, half, j, s, ())
         blend(z + half)
 
         rows_out.wait_send()
-        wait_bytes(w.at[:, pl.ds(0, 2 * half)], ringsend.at[0])
-        wait_bytes(w.at[:, pl.ds(0, 2 * half - 2)], ringsend.at[1])
+        for way, rest in ((0, pl.ds(0, 2)), (1, pl.ds(0, 1))):
+            wait_bytes(w.at[:, pl.ds(0, 2 * half - 2)], ringsend.at[way])
+            wait_bytes(w.at[rest, pl.ds(0, 2)], ringsend.at[way])
         wait_bytes(w.at[:, pl.ds(0, nd - 1)], give)
 
     @pl.when(c == 0)
@@ -326,6 +368,19 @@
         def send_stats(b):
             each(b, lambda d: remote(row, stats.at[z], statsend, statrecv, at(z + d, 0)).start())
 
+        def edges(zz, first, last):
+            @pl.when(z < nz - 1)
+            def _():
+                for k in range(TEAM):
+                    remote(last, acts.at[q, zz, 0], edgesend.at[0], edgerecv,
+                           {"groups": group_at((q + k) % TEAM), "space": z * 2 + 2}).start()
+
+            @pl.when(z > 0)
+            def _():
+                for k in range(TEAM):
+                    remote(first, acts.at[q, zz, 5], edgesend.at[1], edgerecv,
+                           {"groups": group_at((q + k) % TEAM), "space": z * 2 - 1}).start()
+
         def share(zz, src, b):
             for k in range(1, TEAM):
                 remote(src, acts.at[q, zz, middle], partsend, partrecv.at[b],
@@ -336,7 +391,7 @@
 
         for b in range(early + 1):
             send_rows(b)
-        share(z, for_chip(z), 0)
+        share(z, for_chip(z), len(spans))
         hand_over(q, z, cells.at[pl.ds(z * 4 + 1, 3)])
 
         count = float(2 * wide * GROUP)
@@ -355,17 +410,8 @@
             send_rows(k + 1)
             send_stats(k + 1)
 
-        for b in range(len(spans)):
-            wait_bytes(acts.at[0, pl.ds(0, sizes[b]), middle], a2arecv.at[b])
-
-            def body(d):
-                zz = lax.rem(z + d + nz, nz)
-                share(zz, acts.at[q, zz, middle], b)
-                hand_over(q, zz, acts.at[q, zz, norths])
-            each(b, body)
-
         def from_team(b):
-            n = sizes[b] + (1 if b == 0 else 0)
+            n = sizes[b] if b < len(spans) else 1
             wait_bytes(acts.at[pl.ds(0, TEAM - 1), pl.ds(0, n), middle], partrecv.at[b])
 
             def body(d):
@@ -373,40 +419,39 @@
                 for k in range(1, TEAM):
                     p = lax.rem(q + k, TEAM)
                     hand_over(p, zz, acts.at[p, zz, norths])
-            if b == 0:
+            if b < len(spans):
+                each(b, body)
+            else:
                 body(0)
+
+        from_team(len(spans))
+        edges(z, cells.at[z * 4], cells.at[z * 4 + 3])
+        for b in range(len(spans)):
+            if b == len(spans) - 1:
+                wait_bytes(stats.at[pl.ds(0, nz - 1)], statrecv)
+                every = stats[...].reshape(nz, LANES)
+                lane = lax.broadcasted_iota(jnp.int32, (nz, LANES), 1)
+                mean = jnp.sum(every, axis=0, keepdims=True) * (1.0 / (count * nz))
+                off = jnp.where(lane < 32, (every * (1.0 / count) - mean) ** 2 * count, 0.0)
+                spread = jnp.where(lane < 32, 0.0, every)
+                spread = jnp.sum(spread + pltpu.roll(off, 32, 1), axis=0, keepdims=True) * (1.0 / (count * nz))
+                tot[...] = jnp.where(lane[:1] < 32, mean, spread)
+                totals[q] = tot[...]
+                for k in range(1, TEAM):
+                    remote(tot, totals.at[q], totsend.at[0], totrecv.at[0],
+                           {"groups": group_at((q + k) % TEAM)}).start()
+            wait_bytes(acts.at[0, pl.ds(0, sizes[b]), middle], a2arecv.at[b])
+
+            def body(d):
+                zz = lax.rem(z + d + nz, nz)
+                share(zz, acts.at[q, zz, middle], b)
+                edges(zz, acts.at[q, zz, 1], acts.at[q, zz, 4])
+                hand_over(q, zz, acts.at[q, zz, norths])
             each(b, body)
 
-        from_team(0)
-        for k in range(TEAM):
-            g = group_at((q + k) % TEAM)
-
-            @pl.when(z < nz - 1)
-            def _():
-                remote(acts.at[q, :, 4], acts.at[q, :, 0], edgesend.at[0], edgerecv,
-                       {"groups": g, "space": z * 2 + 2}).start()
-
-            @pl.when(z > 0)
-            def _():
-                remote(acts.at[q, :, 1], acts.at[q, :, 5], edgesend.at[1], edgerecv,
-                       {"groups": g, "space": z * 2 - 1}).start()
-
-        wait_bytes(stats.at[pl.ds(0, nz - 1)], statrecv)
-        every = stats[...].reshape(nz, LANES)
-        lane = lax.broadcasted_iota(jnp.int32, (nz, LANES), 1)
-        mean = jnp.sum(every, axis=0, keepdims=True) * (1.0 / (count * nz))
-        off = jnp.where(lane < 32, (every * (1.0 / count) - mean) ** 2 * count, 0.0)
-        spread = jnp.where(lane < 32, 0.0, every)
-        spread = jnp.sum(spread + pltpu.roll(off, 32, 1), axis=0, keepdims=True) * (1.0 / (count * nz))
-        tot[...] = jnp.where(lane[:1] < 32, mean, spread)
-        totals[q] = tot[...]
-        for k in range(1, TEAM):
-            remote(tot, totals.at[q], totsend.at[0], totrecv.at[0],
-                   {"groups": group_at((q + k) % TEAM)}).start()
         wait_bytes(totals.at[pl.ds(0, TEAM - 1)], totrecv.at[0])
         remote(totals, totals, totsend.at[1], totrecv.at[1], sibling).start()
-
-        for b in range(1, len(spans)):
+        for b in range(len(spans)):
             from_team(b)
 
         @pl.when(z > 0)
@@ -417,7 +462,10 @@
         def _():
             acts[:, :, 0] = acts[:, :, 1]
 
-        activate()
+        for copy in small:
+            copy.wait()
+        activate(range(TEAM))
+        arrange()
         wait_bytes(w.at[:, 0], giverecv.at[half])
         blend(z)
 
@@ -431,17 +479,26 @@
         blend(z - NEAR)
         blend(z + NEAR)
 
-        @pl.loop(1, leaps - 1)
+        @pl.loop(1, leaps)
         def _(u):
             wait_bytes(w.at[:, pl.ds(0, 8)], giverecv.at[NEAR - 1 + u])
             for d in (0, -1):
                 blend(z - NEAR - 2 * u - d)
                 blend(z + NEAR + 2 * u + d)
 
-        wait_bytes(w.at[:, pl.ds(0, 10)], giverecv.at[NEAR - 2 + leaps])
-        for d in (half - 2, half - 1):
-            blend(z - d)
-            blend(z + d)
+            @pl.when(u >= leaps - 2)
+            def _():
+                @pl.when(u == leaps - 2)
+                def _():
+                    multiply(0, 0)
+
+                @pl.when(u == leaps - 1)
+                def _():
+                    multiply(1, 0)
+
+        wait_bytes(w.at[:, pl.ds(0, 6)], giverecv.at[NEAR - 1 + leaps])
+        blend(z - half + 1)
+        blend(z + half - 1)
         blend(z + half)
         for p in pieces:
             p.wait_send()
@@ -461,41 +518,20 @@
         wait_bytes(totals, totsend.at[1])
 
     frame = lax.broadcasted_iota(jnp.int32, (8, LANES), 0) % FRAMES
-    few = ROWS // 2
+    which = lax.broadcasted_iota(jnp.int32, (tiles, LANES), 0)
+    bias_row = jnp.sum(jnp.where(which == q, bias[...].astype(F32), 0.0), axis=0, keepdims=True)
     for h in range(2):
-        for dt in (2, 1, 0):
-            dst = total if dt == 2 else acc
-            col0 = 0
-            for dr, dc in SHIFTS:
-                ps = phases_of(dr, dc)
-                lhs = a[1 + dr + h * few:1 + dr + (h + 1) * few, 1 + dc:3 + dc].reshape(few * 2 * 16, channels)
-                r = jnp.dot(lhs, mix[dt, :, col0:col0 + len(ps) * LANES], preferred_element_type=F32)
-                col0 += len(ps) * LANES
-                if (dr, dc) == (0, 0):
-                    dst[...] = r
-                else:
-                    for n, (pr, pc) in enumerate(ps):
-                        cols = slice((pr * 2 + pc) * LANES, (pr * 2 + pc + 1) * LANES)
-                        dst[:, cols] += r[:, n * LANES:(n + 1) * LANES]
-            if dt != 2:
-                @pl.loop(0, acc.shape[0] // 8)
-                def _(i):
-                    rows = pl.ds(pl.multiple_of(i * 8, 8), 8)
-                    for n in range(4):
-                        cols = slice(n * LANES, (n + 1) * LANES)
-                        v = acc[rows, cols]
-                        moved = jnp.where(frame >= 1, pltpu.roll(v, 1, 0), v)
-                        if dt == 0:
-                            moved = jnp.where(frame >= 2, pltpu.roll(v, 2, 0), moved)
-                        total[rows, cols] += moved
-
-        bias_row = bias[q]
+        multiply(h, 1)
         for r in range(few):
             for cc in range(2):
                 for n in range(4):
-                    pr, pc = n // 2, n % 2
-                    i = ((r * 2 + pr) * 2 + cc) * 2 + pc
-                    turn[i * TROWS:i * TROWS + 16] = total[(r * 2 + cc) * 16:(r * 2 + cc + 1) * 16, n * LANES:(n + 1) * LANES] + bias_row
+                    i = ((r * 2 + n // 2) * 2 + cc) * 2 + n % 2
+                    for half_tile in range(2):
+                        at_row = (r * 2 + cc) * 16 + half_tile * 8
+                        old, mid, new = (acc[h, dt, at_row:at_row + 8, n * LANES:(n + 1) * LANES] for dt in range(3))
+                        mid = jnp.where(frame >= 1, pltpu.roll(mid, 1, 0), mid)
+                        old = jnp.where(frame >= 2, pltpu.roll(old, 2, 0), jnp.where(frame >= 1, pltpu.roll(old, 1, 0), old))
+                        turn[i * TROWS + half_tile * 8:i * TROWS + half_tile * 8 + 8] = old + mid + new + bias_row
         put = slice(h * ROWS, (h + 1) * ROWS)
         for p in range(TEAM):
             for f in range(FRAMES):
@@ -522,7 +558,8 @@
     cin = conv_weight.shape[3]
     batches = len(rounds_of(nz // 2)) + 1
     wq = conv_weight.reshape(3, TAPS, cin, conv_weight.shape[4])
-    scratch = [pltpu.VMEM((tiles, 1, LANES), F32)] * 3 + [
+    scratch = [pltpu.VMEM((tiles, 1, LANES), F32)] * 2 + [
+        pltpu.VMEM((tiles, LANES), BF16),
         pltpu.VMEM((3, nd, TAPS, cin, LANES), BF16),
         pltpu.VMEM((3, channels, 16 * LANES), BF16),
         pltpu.VMEM((TEAM, nz, 6, 8, LANES), BF16),
@@ -535,23 +572,23 @@
         pltpu.VMEM((1, LANES), F32),
         pltpu.VMEM((ROWS // 2 * 16 * YROWS, LANES), F32),
         pltpu.VMEM((ROWS + 2, 4, 16, channels), BF16),
-        pltpu.VMEM((ROWS * 16, 4 * LANES), F32),
-        pltpu.VMEM((ROWS * 16, 4 * LANES), F32),
+        pltpu.VMEM((2, 3, ROWS * 16, 4 * LANES), F32),
         pltpu.VMEM((ROWS * 4 * TROWS, LANES), F32),
         pltpu.VMEM((TEAM, FRAMES, ROWS * 2, 4, LANES), BF16),
         DMA((5,)), DMA((2,)), DMA((2, nz // 2, 3)), DMA, DMA((nz // 2 + 1,)), DMA((2, 4)),
         pltpu.SemaphoreType.REGULAR((max(1, batches - 1),)),
-        DMA, DMA((batches,)), DMA, DMA, DMA, DMA((batches,)), DMA, DMA, DMA((2,)), DMA, DMA((2,)), DMA((2,)), DMA, DMA,
+        DMA, DMA((batches,)), DMA, DMA, DMA, DMA((batches + 1,)), DMA, DMA, DMA((2,)), DMA, DMA((2,)), DMA((2,)), DMA, DMA,
     ]
+    operands = (hidden, wq, norm_gain.reshape(tiles, 1, LANES), norm_shift.reshape(tiles, 1, LANES), conv_bias.reshape(tiles, LANES))
     return pl.pallas_call(
         functools.partial(kernel, ny, nd),
-        out_shape=jax.ShapeDtypeStruct((FRAMES, ROWS * 2, 4, channels), BF16),
+        out_shape=pltpu.VMEM((FRAMES, ROWS * 2, 4, channels), BF16),
         in_specs=[HBM] * 5,
         out_specs=VMEM,
         scratch_shapes=scratch,
-        compiler_params=pltpu.CompilerParams(collective_id=0, has_side_effects=True, vmem_limit_bytes=56 * MIB),
+        compiler_params=pltpu.CompilerParams(collective_id=0, has_side_effects=True, vmem_limit_bytes=40 * MIB),
         name="decode",
-    )(hidden, wq, norm_gain.reshape(tiles, 1, LANES), norm_shift.reshape(tiles, 1, LANES), conv_bias.astype(F32).reshape(tiles, 1, LANES))
+    )(*(pltpu.with_memory_space_constraint(v, pltpu.HBM) for v in operands))
 
 
 def solution(mesh):

time: 88.8 us -> 83.1 us (0.936)
  Pallas kernels: 85.4 us -> 81.7 us
  local copies, waits for them, and re-layouts: 2.69 us -> 0.8 us
    pallas_call x1, Pallas kernels: 85.4 us -> 81.7 us  [shards(): pl.pallas_call(functools.partial(kernel, ny, nd), out_shape=pltpu.VMEM((F...]
    unnamed x3 -> x1, local copies, waits for them, and re-layouts: 2.69 us -> 0.8 us
where the time goes in v4:
time: 83.1 us; the launch traced here: 82.5 us
  Pallas kernels  81.7 us (98%)
    pallas_call x1, Pallas kernels, shards(): pl.pallas_call(functools.partial(kernel, ny, nd), out_shape=pltpu.VMEM((F...  81.7 us

profile of v4, /device:TPU:37, one launch (start us, length us, event | category | flops | bytes accessed | tf_op | source)
XLA Modules:
  0.0 82.5 jit_solution(7632352477531114637)
XLA Ops:
  0.0 81.7 %decode.1 = bf16[4,32,4,512]{3,2,1,0:T(4,128)(2,1)S(1)} custom-call(bf16[128,512]{1,0:T(8,128)(2,1)} %h_ref.1, bf16[3,9,8,512]{3,2,1,0:T(8,128)(2,1)} %bitcast.4, f32[4,1,128]{2,1,0:T(1,128)} %bitcast.5, f32[4,1,128]{2,1,0:T(1,128)} %bitcast.6, bf16[4,128]{1,0:T(4,128)(2,1)} %bitcast.7), custom_call_target="tpu_custom_call" | custom-call | tf_op jit(solution)/shard_map/decode/pallas_call | solution.py:583
  81.7 0.8 copy.7

commit v5 on v4

--- a/solution.py
+++ b/solution.py
@@ -14,6 +14,7 @@
 TEAM = 4
 TAPS = 9
 EPSILON = 1e-6
+PARTS = (4, 4, 4, 4)
 MIB = 1 << 20
 YROWS = 40
 TROWS = 24
@@ -51,7 +52,9 @@
     g = lax.axis_index("groups")
     x, y = g // ny, g % ny
     x0, y0 = x - x % 2, y - y % 2
-    return (x % 2) * 2 + y % 2, lambda p: (x0 + p // 2) * ny + y0 + p % 2
+    q = (x % 2) * 2 + y % 2
+    others = (3 - q, (q + 2) % TEAM, q + 1 - 2 * (q % 2))
+    return q, others, lambda p: (x0 + p // 2) * ny + y0 + p % 2
 
 
 def group_matrix():
@@ -91,12 +94,12 @@
 def kernel(ny, nd, h_ref, wq_ref, gain_ref, shift_ref, bias_ref, out, gain, shift, bias,
            w, mix, acts, totals, raw, cells, flat, stats, row, tot, ys, a, acc, turn, mine,
            local, ringsend, ringrecv, give, giverecv, own, ask, a2asend, a2arecv,
-           statsend, statrecv, partsend, partrecv, northsend, northrecv, edgesend, edgerecv, totsend, totrecv, outsend, outrecv):
+           statsend, statrecv, partsend, partrecv, northsend, northrecv, edgesend, edgerecv, outersend, outerrecv, totsend, totrecv, outsend, outrecv):
     me = lax.axis_index("space")
     z, c = me // 2, me % 2
     nz = nd // 2
     half = nz // 2
-    q, group_at = team(ny)
+    q, others, group_at = team(ny)
     leaps = (half - NEAR) // 2
     assert NEAR + 2 * leaps == half
     rounds = rounds_of(half)
@@ -110,6 +113,8 @@
         return {"space": lax.rem(zz + 2 * nz, nz) * 2 + core}
 
     sibling = {"space": z * 2 + 1 - c}
+    middle = pl.ds(1, 4)
+    norths = pl.ds(2, 3)
     barrier = pltpu.get_barrier_semaphore()
 
     def blend(zz):
@@ -141,7 +146,7 @@
             @pl.loop(0, pairs, unroll=4)
             def _(rp):
                 for f in range(FRAMES):
-                    v = acts[p, f * pairs + rp, pl.ds(2 * c, 4)].astype(F32)
+                    v = acts[p, lax.rem(f * pairs + rp + nz - z, nz), pl.ds(2 * c, 4)].astype(F32)
                     v = v * scale[None] + move[None]
                     v = v * jnp.tanh(v) + v
                     start = rp * (16 * YROWS) + (p * FRAMES + f) * YROWS
@@ -159,28 +164,28 @@
         a[0] = a[1]
         a[ROWS + 1] = a[ROWS]
 
-    few = ROWS // 2
     chips = LANES // 16
     first_block = z // chips + jnp.where(z % chips < chips // 2, tiles - 1, 0)
     assert half - 4 >= chips * 3 // 2 - 1 and tiles == 4
 
-    def multiply(h, late):
+    def multiply(row0, few, late):
+        part = slice(row0 * 32, (row0 + few) * 32)
         blocks = [pl.ds(pl.multiple_of(lax.rem(first_block + 2 * late + i, tiles) * LANES, LANES), LANES) for i in range(2)]
         for dt in range(3):
             col0 = 0
             for dr, dc in SHIFTS:
                 ps = phases_of(dr, dc)
-                rows, cols = slice(1 + dr + h * few, 1 + dr + (h + 1) * few), slice(1 + dc, 3 + dc)
+                rows, cols = slice(1 + dr + row0, 1 + dr + row0 + few), slice(1 + dc, 3 + dc)
                 lhs = jnp.concatenate([a[rows, cols, :, k].reshape(few * 2 * 16, LANES) for k in blocks], axis=1)
                 rhs = jnp.concatenate([mix[dt, k, col0:col0 + len(ps) * LANES] for k in blocks], axis=0)
                 r = jnp.dot(lhs, rhs, preferred_element_type=F32)
                 col0 += len(ps) * LANES
                 if (dr, dc) == (0, 0):
-                    acc[h, dt] = acc[h, dt] + r if late else r
+                    acc[dt, part] = acc[dt, part] + r if late else r
                 else:
                     for n, (pr, pc) in enumerate(ps):
                         to = slice((pr * 2 + pc) * LANES, (pr * 2 + pc + 1) * LANES)
-                        acc[h, dt, :, to] += r[:, n * LANES:(n + 1) * LANES]
+                        acc[dt, part, to] += r[:, n * LANES:(n + 1) * LANES]
 
     load = pltpu.make_async_copy(wq_ref.at[:, :, :, pl.ds(q * LANES, LANES)], w.at[:, me], local.at[0])
     rows_in = pltpu.make_async_copy(h_ref, raw.at[0], local.at[1])
@@ -254,7 +259,7 @@
 
                 @pl.when(z < nz - 1)
                 def _():
-                    wait_bytes(acts.at[:, :, 5], edgerecv)
+                    wait_bytes(acts.at[:, :, 5], outerrecv)
 
                 @pl.when(z == nz - 1)
                 def _():
@@ -285,8 +290,8 @@
             take(1, d - 1, j, s, ())
         blend(z - d + 1)
         blend(z + d - 1)
-        multiply(0, 0)
-        multiply(1, 0)
+        multiply(0, ROWS // 2, 0)
+        multiply(ROWS // 2, ROWS // 2, 0)
         s = NEAR - 1 + leaps
         for j in range(3):
             take(0, half - 1, j, s, ())
@@ -296,20 +301,14 @@
         for j in range(3):
             take(0 if j < 2 else 1, half, j, s, ())
         blend(z + half)
-
-        rows_out.wait_send()
-        for way, rest in ((0, pl.ds(0, 2)), (1, pl.ds(0, 1))):
-            wait_bytes(w.at[:, pl.ds(0, 2 * half - 2)], ringsend.at[way])
-            wait_bytes(w.at[rest, pl.ds(0, 2)], ringsend.at[way])
-        wait_bytes(w.at[:, pl.ds(0, nd - 1)], give)
 
     @pl.when(c == 0)
     def _():
         signal(barrier, at(z + 1, 0))
         signal(barrier, at(z - 1, 0))
         signal(barrier, sibling)
-        for k in range(1, TEAM):
-            signal(barrier, {"groups": group_at((q + k) % TEAM)})
+        for p in others:
+            signal(barrier, {"groups": group_at(p)})
         load.start()
         rows_in.start()
         for copy in small:
@@ -323,11 +322,9 @@
 
         tell(0)
         load.wait()
-        pieces = []
         for j in range(3):
             p = w.at[j, me]
-            pieces.append(remote(p, p, own.at[0, 1 + j], own.at[1, 1 + j], sibling))
-            pieces[-1].start()
+            remote(p, p, own.at[0, 1 + j], own.at[1, 1 + j], sibling).start()
         early = min(2, len(rounds))
         for k in range(early):
             pl.semaphore_wait(ask.at[k], 2)
@@ -353,8 +350,12 @@
             if hi == half:
                 body(half)
 
-        middle = pl.ds(1, 4)
-        norths = pl.ds(2, 3)
+        def runs(b):
+            if b == len(spans):
+                return [(0, 1)]
+            lo, hi = spans[b]
+            low = min(hi, half - 1)
+            return [(lo, hi - lo + 1), (nz - low, low - lo + 1)]
 
         def for_chip(zz):
             return cells.at[pl.ds(zz * 4, 4)]
@@ -362,37 +363,52 @@
         def send_rows(b):
             def body(d):
                 zz = lax.rem(z + d + nz, nz)
-                remote(for_chip(zz), acts.at[q, z, middle], a2asend, a2arecv.at[b], at(zz, 0)).start()
+                remote(for_chip(zz), acts.at[q, lax.rem(nz - d, nz), middle], a2asend, a2arecv.at[b], at(zz, 0)).start()
             each(b, body)
 
         def send_stats(b):
             each(b, lambda d: remote(row, stats.at[z], statsend, statrecv, at(z + d, 0)).start())
 
-        def edges(zz, first, last):
+        def pass_on(b, at0, n, rows, first, last):
+            for p in others:
+                remote(rows(middle), acts.at[q, pl.ds(at0, n), middle], partsend, partrecv.at[b], {"groups": group_at(p)}).start()
+
             @pl.when(z < nz - 1)
             def _():
-                for k in range(TEAM):
-                    remote(last, acts.at[q, zz, 0], edgesend.at[0], edgerecv,
-                           {"groups": group_at((q + k) % TEAM), "space": z * 2 + 2}).start()
+                remote(last, acts.at[q, pl.ds((at0 + nz - 1) % nz, n), 0], edgesend.at[0], edgerecv.at[0, b], at(z + 1, 0)).start()
 
             @pl.when(z > 0)
             def _():
-                for k in range(TEAM):
-                    remote(first, acts.at[q, zz, 5], edgesend.at[1], edgerecv,
-                           {"groups": group_at((q + k) % TEAM), "space": z * 2 - 1}).start()
-
-        def share(zz, src, b):
-            for k in range(1, TEAM):
-                remote(src, acts.at[q, zz, middle], partsend, partrecv.at[b],
-                       {"groups": group_at((q + k) % TEAM)}).start()
-
-        def hand_over(p, zz, src):
-            remote(src, acts.at[p, zz, norths], northsend, northrecv, sibling).start()
+                remote(first, acts.at[q, pl.ds((at0 + 1) % nz, n), 5], edgesend.at[1], edgerecv.at[1, b], at(z - 1, 0)).start()
+
+            remote(rows(norths), acts.at[q, pl.ds(at0, n), norths], northsend, northrecv, sibling).start()
+
+        def share_edges(b):
+            total = sum(n for _, n in runs(b))
+
+            @pl.when(z > 0)
+            def _():
+                wait_bytes(acts.at[0, pl.ds(0, total), 0], edgerecv.at[0, b])
+                for at0, n in runs(b):
+                    e = acts.at[q, pl.ds((at0 + nz - 1) % nz, n), 0]
+                    for p in others:
+                        remote(e, e, outersend.at[0], outerrecv, {"groups": group_at(p)}).start()
+
+            @pl.when(z < nz - 1)
+            def _():
+                wait_bytes(acts.at[0, pl.ds(0, total), 5], edgerecv.at[1, b])
+                for at0, n in runs(b):
+                    e = acts.at[q, pl.ds((at0 + 1) % nz, n), 5]
+                    for p in others:
+                        remote(e, e, outersend.at[1], outerrecv, {"groups": group_at(p), "space": z * 2 + 1}).start()
+                    remote(e, e, outersend.at[1], outerrecv, sibling).start()
 
         for b in range(early + 1):
             send_rows(b)
-        share(z, for_chip(z), len(spans))
-        hand_over(q, z, cells.at[pl.ds(z * 4 + 1, 3)])
+        own_cells = len(spans)
+        for p in others:
+            remote(for_chip(z), acts.at[q, 0, middle], partsend, partrecv.at[own_cells], {"groups": group_at(p)}).start()
+        remote(cells.at[pl.ds(z * 4 + 1, 3)], acts.at[q, 0, norths], northsend, northrecv, sibling).start()
 
         count = float(2 * wide * GROUP)
         first = pack(jnp.sum(flat[...].reshape(wide, 8, LANES), axis=0), 0)
@@ -400,7 +416,7 @@
         second = pack(jnp.sum((flat[...].reshape(wide, 8, LANES) - mean[None]) ** 2, axis=0), 1)
         row[...] = first + second
         stats[z] = row[...]
-        acts[q, z, 1:5] = cells[pl.ds(z * 4, 4)]
+        acts[q, 0, 1:5] = cells[pl.ds(z * 4, 4)]
         for b in range(early + 1):
             send_stats(b)
 
@@ -411,21 +427,24 @@
             send_stats(k + 1)
 
         def from_team(b):
-            n = sizes[b] if b < len(spans) else 1
-            wait_bytes(acts.at[pl.ds(0, TEAM - 1), pl.ds(0, n), middle], partrecv.at[b])
-
-            def body(d):
-                zz = lax.rem(z + d + nz, nz)
-                for k in range(1, TEAM):
-                    p = lax.rem(q + k, TEAM)
-                    hand_over(p, zz, acts.at[p, zz, norths])
-            if b < len(spans):
-                each(b, body)
-            else:
-                body(0)
-
-        from_team(len(spans))
-        edges(z, cells.at[z * 4], cells.at[z * 4 + 3])
+            total = sum(n for _, n in runs(b))
+            wait_bytes(acts.at[pl.ds(0, TEAM - 1), pl.ds(0, total), middle], partrecv.at[b])
+            for at0, n in runs(b):
+                for p in others:
+                    c3 = acts.at[p, pl.ds(at0, n), norths]
+                    remote(c3, c3, northsend, northrecv, sibling).start()
+
+        from_team(own_cells)
+
+        @pl.when(z < nz - 1)
+        def _():
+            remote(cells.at[z * 4 + 3], acts.at[q, nz - 1, 0], edgesend.at[0], edgerecv.at[0, own_cells], at(z + 1, 0)).start()
+
+        @pl.when(z > 0)
+        def _():
+            remote(cells.at[z * 4], acts.at[q, 1, 5], edgesend.at[1], edgerecv.at[1, own_cells], at(z - 1, 0)).start()
+
+        share_edges(own_cells)
         for b in range(len(spans)):
             if b == len(spans) - 1:
                 wait_bytes(stats.at[pl.ds(0, nz - 1)], statrecv)
@@ -437,26 +456,26 @@
                 spread = jnp.sum(spread + pltpu.roll(off, 32, 1), axis=0, keepdims=True) * (1.0 / (count * nz))
                 tot[...] = jnp.where(lane[:1] < 32, mean, spread)
                 totals[q] = tot[...]
-                for k in range(1, TEAM):
-                    remote(tot, totals.at[q], totsend.at[0], totrecv.at[0],
-                           {"groups": group_at((q + k) % TEAM)}).start()
+                for p in others:
+                    remote(tot, totals.at[q], totsend.at[0], totrecv.at[0], {"groups": group_at(p)}).start()
             wait_bytes(acts.at[0, pl.ds(0, sizes[b]), middle], a2arecv.at[b])
 
-            def body(d):
-                zz = lax.rem(z + d + nz, nz)
-                share(zz, acts.at[q, zz, middle], b)
-                edges(zz, acts.at[q, zz, 1], acts.at[q, zz, 4])
-                hand_over(q, zz, acts.at[q, zz, norths])
-            each(b, body)
+            for at0, n in runs(b):
+                pass_on(b, at0, n, lambda cols, at0=at0, n=n: acts.at[q, pl.ds(at0, n), cols],
+                        acts.at[q, pl.ds(at0, n), 1], acts.at[q, pl.ds(at0, n), 4])
+            if b > 0:
+                share_edges(b - 1)
 
         wait_bytes(totals.at[pl.ds(0, TEAM - 1)], totrecv.at[0])
         remote(totals, totals, totsend.at[1], totrecv.at[1], sibling).start()
-        for b in range(len(spans)):
+        for b in range(len(spans) - 1):
             from_team(b)
+        share_edges(len(spans) - 1)
+        from_team(len(spans) - 1)
 
         @pl.when(z > 0)
         def _():
-            wait_bytes(acts.at[:, :, 0], edgerecv)
+            wait_bytes(acts.at[pl.ds(0, TEAM - 1), :, 0], outerrecv)
 
         @pl.when(z == 0)
         def _():
@@ -490,58 +509,72 @@
             def _():
                 @pl.when(u == leaps - 2)
                 def _():
-                    multiply(0, 0)
+                    multiply(0, ROWS // 2, 0)
 
                 @pl.when(u == leaps - 1)
                 def _():
-                    multiply(1, 0)
+                    multiply(ROWS // 2, ROWS // 2, 0)
 
         wait_bytes(w.at[:, pl.ds(0, 6)], giverecv.at[NEAR - 1 + leaps])
         blend(z - half + 1)
         blend(z + half - 1)
         blend(z + half)
-        for p in pieces:
-            p.wait_send()
-        wait_bytes(stats.at[pl.ds(0, nz - 1)], statsend)
-        wait_bytes(acts.at[0, pl.ds(0, nz - 1), middle], a2asend)
-        wait_bytes(acts.at[pl.ds(0, TEAM - 1), :, middle], partsend)
-        wait_bytes(acts.at[:, :, norths], northsend)
-
-        @pl.when(z < nz - 1)
-        def _():
-            wait_bytes(acts.at[:, :, 0], edgesend.at[0])
-
-        @pl.when(z > 0)
-        def _():
-            wait_bytes(acts.at[:, :, 0], edgesend.at[1])
-        wait_bytes(totals.at[pl.ds(0, TEAM - 1)], totsend.at[0])
-        wait_bytes(totals, totsend.at[1])
 
     frame = lax.broadcasted_iota(jnp.int32, (8, LANES), 0) % FRAMES
     which = lax.broadcasted_iota(jnp.int32, (tiles, LANES), 0)
     bias_row = jnp.sum(jnp.where(which == q, bias[...].astype(F32), 0.0), axis=0, keepdims=True)
-    for h in range(2):
-        multiply(h, 1)
+    row0 = 0
+    for few in PARTS:
+        multiply(row0, few, 1)
         for r in range(few):
             for cc in range(2):
                 for n in range(4):
                     i = ((r * 2 + n // 2) * 2 + cc) * 2 + n % 2
                     for half_tile in range(2):
-                        at_row = (r * 2 + cc) * 16 + half_tile * 8
-                        old, mid, new = (acc[h, dt, at_row:at_row + 8, n * LANES:(n + 1) * LANES] for dt in range(3))
+                        at_row = ((row0 + r) * 2 + cc) * 16 + half_tile * 8
+                        old, mid, new = (acc[dt, at_row:at_row + 8, n * LANES:(n + 1) * LANES] for dt in range(3))
                         mid = jnp.where(frame >= 1, pltpu.roll(mid, 1, 0), mid)
                         old = jnp.where(frame >= 2, pltpu.roll(old, 2, 0), jnp.where(frame >= 1, pltpu.roll(old, 1, 0), old))
                         turn[i * TROWS + half_tile * 8:i * TROWS + half_tile * 8 + 8] = old + mid + new + bias_row
-        put = slice(h * ROWS, (h + 1) * ROWS)
+        put = slice(row0 * 2, (row0 + few) * 2)
+        row0 += few
         for p in range(TEAM):
             for f in range(FRAMES):
                 v = turn[pl.ds(p * FRAMES + f, few * 8, stride=TROWS)].astype(BF16)
-                mine[p, f, put] = v.reshape(ROWS, 4, LANES)
+                mine[p, f, put] = v.reshape(few * 2, 4, LANES)
         here = pl.ds(pl.multiple_of(q * LANES, LANES), LANES)
-        for k in (3, 2, 1):
-            p = lax.rem(q + k, TEAM)
+        for p in others:
             remote(mine.at[p, :, put], out.at[:, put, :, here], outsend, outrecv, {"groups": group_at(p)}).start()
         out[:, put, :, here] = mine[q, :, put]
+    @pl.when(c == 1)
+    def _():
+        wait_bytes(raw.at[0], own.at[0, 0])
+        for way, rest in ((0, pl.ds(0, 2)), (1, pl.ds(0, 1))):
+            wait_bytes(w.at[:, pl.ds(0, 2 * half - 2)], ringsend.at[way])
+            wait_bytes(w.at[rest, pl.ds(0, 2)], ringsend.at[way])
+        wait_bytes(w.at[:, pl.ds(0, nd - 1)], give)
+
+    @pl.when(c == 0)
+    def _():
+        for j in range(3):
+            wait_bytes(w.at[j, me], own.at[0, 1 + j])
+        wait_bytes(stats.at[pl.ds(0, nz - 1)], statsend)
+        wait_bytes(acts.at[0, pl.ds(0, nz - 1), middle], a2asend)
+        wait_bytes(acts.at[pl.ds(0, TEAM - 1), :, middle], partsend)
+        wait_bytes(acts.at[:, :, norths], northsend)
+
+        @pl.when(z < nz - 1)
+        def _():
+            wait_bytes(acts.at[0, :, 0], edgesend.at[0])
+            wait_bytes(acts.at[:, :, 5], outersend.at[1])
+
+        @pl.when(z > 0)
+        def _():
+            wait_bytes(acts.at[0, :, 5], edgesend.at[1])
+            wait_bytes(acts.at[pl.ds(0, TEAM - 1), :, 0], outersend.at[0])
+        wait_bytes(totals.at[pl.ds(0, TEAM - 1)], totsend.at[0])
+        wait_bytes(totals, totsend.at[1])
+
     wait_bytes(mine.at[pl.ds(0, TEAM - 1)], outrecv)
     wait_bytes(mine.at[pl.ds(0, TEAM - 1)], outsend)
 
@@ -572,12 +605,12 @@
         pltpu.VMEM((1, LANES), F32),
         pltpu.VMEM((ROWS // 2 * 16 * YROWS, LANES), F32),
         pltpu.VMEM((ROWS + 2, 4, 16, channels), BF16),
-        pltpu.VMEM((2, 3, ROWS * 16, 4 * LANES), F32),
+        pltpu.VMEM((3, ROWS * 32, 4 * LANES), F32),
         pltpu.VMEM((ROWS * 4 * TROWS, LANES), F32),
         pltpu.VMEM((TEAM, FRAMES, ROWS * 2, 4, LANES), BF16),
         DMA((5,)), DMA((2,)), DMA((2, nz // 2, 3)), DMA, DMA((nz // 2 + 1,)), DMA((2, 4)),
         pltpu.SemaphoreType.REGULAR((max(1, batches - 1),)),
-        DMA, DMA((batches,)), DMA, DMA, DMA, DMA((batches + 1,)), DMA, DMA, DMA((2,)), DMA, DMA((2,)), DMA((2,)), DMA, DMA,
+        DMA, DMA((batches,)), DMA, DMA, DMA, DMA((batches + 1,)), DMA, DMA, DMA((2,)), DMA((2, batches + 1)), DMA((2,)), DMA, DMA((2,)), DMA((2,)), DMA, DMA,
     ]
     operands = (hidden, wq, norm_gain.reshape(tiles, 1, LANES), norm_shift.reshape(tiles, 1, LANES), conv_bias.reshape(tiles, LANES))
     return pl.pallas_call(

time: 83.1 us -> 79.6 us (0.958)
  Pallas kernels: 81.7 us -> 78.7 us
    pallas_call x1, Pallas kernels: 81.7 us -> 78.7 us  [shards(): pl.pallas_call(functools.partial(kernel, ny, nd), out_shape=pltpu.VMEM((F...]
where the time goes in v5:
time: 79.6 us; the launch traced here: 79.5 us
  Pallas kernels  78.7 us (99%)
  local copies, waits for them, and re-layouts  0.8 us (1%)
    pallas_call x1, Pallas kernels, shards(): pl.pallas_call(functools.partial(kernel, ny, nd), out_shape=pltpu.VMEM((F...  78.7 us

profile of v5, /device:TPU:37, one launch (start us, length us, event | category | flops | bytes accessed | tf_op | source)
XLA Modules:
  0.0 79.5 jit_solution(930015980554044135)
XLA Ops:
  0.0 78.7 %decode.1 = bf16[4,32,4,512]{3,2,1,0:T(4,128)(2,1)S(1)} custom-call(bf16[128,512]{1,0:T(8,128)(2,1)} %h_ref.1, bf16[3,9,8,512]{3,2,1,0:T(8,128)(2,1)} %bitcast.4, f32[4,1,128]{2,1,0:T(1,128)} %bitcast.5, f32[4,1,128]{2,1,0:T(1,128)} %bitcast.6, bf16[4,128]{1,0:T(4,128)(2,1)} %bitcast.7), custom_call_target="tpu_custom_call" | custom-call | tf_op jit(solution)/shard_map/decode/pallas_call | solution.py:616
  78.7 0.8 %copy.7 = bf16[4,32,4,512]{3,2,1,0:T(4,128)(2,1)} copy(bf16[4,32,4,512]{3,2,1,0:T(4,128)(2,1)S(1)} %decode.1) | data formatting | bytes 1048576

commit v6 on v5

--- a/solution.py
+++ b/solution.py
@@ -140,14 +140,13 @@
         for p in places:
             mean = unpack(totals[p], 0)
             scale = g * lax.rsqrt(unpack(totals[p], 1) + EPSILON)
-            move = (b - mean * scale) * 0.5
-            scale = scale * 0.5
+            scale, move = scale * 0.5, b * 0.5
 
             @pl.loop(0, pairs, unroll=4)
             def _(rp):
                 for f in range(FRAMES):
                     v = acts[p, lax.rem(f * pairs + rp + nz - z, nz), pl.ds(2 * c, 4)].astype(F32)
-                    v = v * scale[None] + move[None]
+                    v = (v - mean[None]) * scale[None] + move[None]
                     v = v * jnp.tanh(v) + v
                     start = rp * (16 * YROWS) + (p * FRAMES + f) * YROWS
                     ys[pl.ds(pl.multiple_of(start, 8), 32)] = v.reshape(32, LANES)
@@ -247,8 +246,11 @@
         def _(u):
             d, s = NEAR + 2 * u, NEAR - 1 + u
             for j in range(3):
-                take(0, d, j, s, (2, 1))
-                take(1, d, j, s, (2, 1))
+                take(0, d, j, s, (2,))
+                take(1, d, j, s, (2,))
+            for j in range(3):
+                hop(0, piece(z - d, j), d + 1, j).start()
+                hop(1, piece(z + d, j), d + 1, j).start()
             blend(z - d)
             blend(z + d)
 
@@ -281,8 +283,11 @@
         arrange()
         d, s = half - 2, NEAR - 2 + leaps
         for j in range(3):
-            take(0, d, j, s, (2, 1) if j < 2 else (1,))
-            take(1, d, j, s, (1,) if j < 2 else (2, 1))
+            take(0, d, j, s, (2,) if j < 2 else ())
+            take(1, d, j, s, () if j < 2 else (2,))
+        for j in range(3):
+            hop(0, piece(z - d, j), d + 1, j).start()
+            hop(1, piece(z + d, j), d + 1, j).start()
         blend(z - d)
         blend(z + d)
         for j in range(3):
@@ -336,7 +341,7 @@
         for r in range(2):
             for t in range(tiles):
                 flat[pl.ds(r * tiles + t, wide, stride=8)] = raw[r, :, t * LANES:(t + 1) * LANES].astype(F32)
-        x = flat[...].reshape(wide, 8, LANES)
+        x = flat[:wide * 8].reshape(wide, 8, LANES)
         cells[...] = x.astype(BF16)
 
         def each(b, body):
@@ -403,6 +408,7 @@
                         remote(e, e, outersend.at[1], outerrecv, {"groups": group_at(p), "space": z * 2 + 1}).start()
                     remote(e, e, outersend.at[1], outerrecv, sibling).start()
 
+        acts[q, 0, 1:5] = cells[pl.ds(z * 4, 4)]
         for b in range(early + 1):
             send_rows(b)
         own_cells = len(spans)
@@ -411,12 +417,11 @@
         remote(cells.at[pl.ds(z * 4 + 1, 3)], acts.at[q, 0, norths], northsend, northrecv, sibling).start()
 
         count = float(2 * wide * GROUP)
-        first = pack(jnp.sum(flat[...].reshape(wide, 8, LANES), axis=0), 0)
+        first = pack(jnp.sum(flat[:wide * 8].reshape(wide, 8, LANES), axis=0), 0)
         mean = unpack(first, 0) * (1.0 / count)
-        second = pack(jnp.sum((flat[...].reshape(wide, 8, LANES) - mean[None]) ** 2, axis=0), 1)
+        second = pack(jnp.sum((flat[:wide * 8].reshape(wide, 8, LANES) - mean[None]) ** 2, axis=0), 1)
         row[...] = first + second
         stats[z] = row[...]
-        acts[q, 0, 1:5] = cells[pl.ds(z * 4, 4)]
         for b in range(early + 1):
             send_stats(b)
 
@@ -543,9 +548,9 @@
                 v = turn[pl.ds(p * FRAMES + f, few * 8, stride=TROWS)].astype(BF16)
                 mine[p, f, put] = v.reshape(few * 2, 4, LANES)
         here = pl.ds(pl.multiple_of(q * LANES, LANES), LANES)
+        out[:, put, :, here] = mine[q, :, put]
         for p in others:
             remote(mine.at[p, :, put], out.at[:, put, :, here], outsend, outrecv, {"groups": group_at(p)}).start()
-        out[:, put, :, here] = mine[q, :, put]
     @pl.when(c == 1)
     def _():
         wait_bytes(raw.at[0], own.at[0, 0])
@@ -599,14 +604,14 @@
         pltpu.VMEM((TEAM, 1, LANES), F32),
         pltpu.VMEM((2, wide, channels), BF16),
         pltpu.VMEM((wide, 8, LANES), BF16),
-        pltpu.VMEM((wide * 8, LANES), F32),
+        pltpu.VMEM((wide * 8 + 8, LANES), F32),
         pltpu.VMEM((nz, 1, LANES), F32),
         pltpu.VMEM((1, LANES), F32),
         pltpu.VMEM((1, LANES), F32),
-        pltpu.VMEM((ROWS // 2 * 16 * YROWS, LANES), F32),
+        pltpu.VMEM((ROWS // 2 * 16 * YROWS + YROWS, LANES), F32),
         pltpu.VMEM((ROWS + 2, 4, 16, channels), BF16),
         pltpu.VMEM((3, ROWS * 32, 4 * LANES), F32),
-        pltpu.VMEM((ROWS * 4 * TROWS, LANES), F32),
+        pltpu.VMEM((max(PARTS) * 8 * TROWS + TROWS, LANES), F32),
         pltpu.VMEM((TEAM, FRAMES, ROWS * 2, 4, LANES), BF16),
         DMA((5,)), DMA((2,)), DMA((2, nz // 2, 3)), DMA, DMA((nz // 2 + 1,)), DMA((2, 4)),
         pltpu.SemaphoreType.REGULAR((max(1, batches - 1),)),

time: 79.6 us -> 79.1 us (level)
  no operation moved by 1% of the time
where the time goes in v6:
time: 79.1 us; the launch traced here: 78.9 us
  Pallas kernels  78.1 us (99%)
  local copies, waits for them, and re-layouts  0.8 us (1%)
    pallas_call x1, Pallas kernels, shards(): pl.pallas_call(functools.partial(kernel, ny, nd), out_shape=pltpu.VMEM((F...  78.1 us

profile of v6, /device:TPU:37, one launch (start us, length us, event | category | flops | bytes accessed | tf_op | source)
XLA Modules:
  0.0 78.9 jit_solution(10576019322512641419)
XLA Ops:
  0.0 78.1 %decode.1 = bf16[4,32,4,512]{3,2,1,0:T(4,128)(2,1)S(1)} custom-call(bf16[128,512]{1,0:T(8,128)(2,1)} %h_ref.1, bf16[3,9,8,512]{3,2,1,0:T(8,128)(2,1)} %bitcast.4, f32[4,1,128]{2,1,0:T(1,128)} %bitcast.5, f32[4,1,128]{2,1,0:T(1,128)} %bitcast.6, bf16[4,128]{1,0:T(4,128)(2,1)} %bitcast.7), custom_call_target="tpu_custom_call" | custom-call | tf_op jit(solution)/shard_map/decode/pallas_call | solution.py:621
  78.1 0.8 %copy.7 = bf16[4,32,4,512]{3,2,1,0:T(4,128)(2,1)} copy(bf16[4,32,4,512]{3,2,1,0:T(4,128)(2,1)S(1)} %decode.1) | data formatting | bytes 1048576

commit v7 on v6

--- a/solution.py
+++ b/solution.py
@@ -93,7 +93,7 @@
 
 def kernel(ny, nd, h_ref, wq_ref, gain_ref, shift_ref, bias_ref, out, gain, shift, bias,
            w, mix, acts, totals, raw, cells, flat, stats, row, tot, ys, a, acc, turn, mine,
-           local, ringsend, ringrecv, give, giverecv, own, ask, a2asend, a2arecv,
+           local, southsend, ringsend, ringrecv, give, giverecv, own, ask, a2asend, a2arecv,
            statsend, statrecv, partsend, partrecv, northsend, northrecv, edgesend, edgerecv, outersend, outerrecv, totsend, totrecv, outsend, outrecv):
     me = lax.axis_index("space")
     z, c = me // 2, me % 2
@@ -193,14 +193,15 @@
 
     @pl.when(c == 1)
     def _():
-        signal(barrier, at(z + 1, 1))
-        signal(barrier, at(z - 1, 1))
+        for d in (1, -1):
+            for core in (1, 0):
+                signal(barrier, at(z + d, core))
         signal(barrier, sibling)
         load.start()
         rows_in.start()
         for copy in small:
             copy.start()
-        pl.semaphore_wait(barrier, 3)
+        pl.semaphore_wait(barrier, 5)
         rows_in.wait()
         rows_out = remote(raw.at[0], raw.at[1], own.at[0, 0], own.at[1, 0], sibling)
         rows_out.start()
@@ -224,7 +225,6 @@
         for j in range(3):
             theirs = w.at[j, z * 2]
             remote(theirs, theirs, own.at[0, 1 + j], own.at[1, 1 + j], sibling).wait_recv()
-            first(theirs, j)
         blend(z)
 
         def take(way, d, j, s, on):
@@ -309,8 +309,9 @@
 
     @pl.when(c == 0)
     def _():
-        signal(barrier, at(z + 1, 0))
-        signal(barrier, at(z - 1, 0))
+        for d in (1, -1):
+            for core in (1, 0):
+                signal(barrier, at(z + d, core))
         signal(barrier, sibling)
         for p in others:
             signal(barrier, {"groups": group_at(p)})
@@ -318,7 +319,7 @@
         rows_in.start()
         for copy in small:
             copy.start()
-        pl.semaphore_wait(barrier, 2 + TEAM)
+        pl.semaphore_wait(barrier, 4 + TEAM)
 
         def tell(k):
             if k < len(rounds):
@@ -327,6 +328,10 @@
 
         tell(0)
         load.wait()
+        for j in range(3):
+            p = w.at[j, me]
+            remote(p, p, southsend, ringrecv.at[0, 0, j], at(z + 1, 1)).start()
+            remote(p, p, southsend, ringrecv.at[1, 0, j], at(z - 1, 1)).start()
         for j in range(3):
             p = w.at[j, me]
             remote(p, p, own.at[0, 1 + j], own.at[1, 1 + j], sibling).start()
@@ -554,15 +559,17 @@
     @pl.when(c == 1)
     def _():
         wait_bytes(raw.at[0], own.at[0, 0])
-        for way, rest in ((0, pl.ds(0, 2)), (1, pl.ds(0, 1))):
-            wait_bytes(w.at[:, pl.ds(0, 2 * half - 2)], ringsend.at[way])
-            wait_bytes(w.at[rest, pl.ds(0, 2)], ringsend.at[way])
+        wait_bytes(w.at[:, pl.ds(0, 2 * half - 2)], ringsend.at[0])
+        wait_bytes(w.at[0, pl.ds(0, 1)], ringsend.at[0])
+        wait_bytes(w.at[:, pl.ds(0, 2 * half - 3)], ringsend.at[1])
+        wait_bytes(w.at[0, pl.ds(0, 2)], ringsend.at[1])
         wait_bytes(w.at[:, pl.ds(0, nd - 1)], give)
 
     @pl.when(c == 0)
     def _():
         for j in range(3):
             wait_bytes(w.at[j, me], own.at[0, 1 + j])
+        wait_bytes(w.at[:, pl.ds(0, 2)], southsend)
         wait_bytes(stats.at[pl.ds(0, nz - 1)], statsend)
         wait_bytes(acts.at[0, pl.ds(0, nz - 1), middle], a2asend)
         wait_bytes(acts.at[pl.ds(0, TEAM - 1), :, middle], partsend)
@@ -613,7 +620,7 @@
         pltpu.VMEM((3, ROWS * 32, 4 * LANES), F32),
         pltpu.VMEM((max(PARTS) * 8 * TROWS + TROWS, LANES), F32),
         pltpu.VMEM((TEAM, FRAMES, ROWS * 2, 4, LANES), BF16),
-        DMA((5,)), DMA((2,)), DMA((2, nz // 2, 3)), DMA, DMA((nz // 2 + 1,)), DMA((2, 4)),
+        DMA((5,)), DMA, DMA((2,)), DMA((2, nz // 2, 3)), DMA, DMA((nz // 2 + 1,)), DMA((2, 4)),
         pltpu.SemaphoreType.REGULAR((max(1, batches - 1),)),
         DMA, DMA((batches,)), DMA, DMA, DMA, DMA((batches + 1,)), DMA, DMA, DMA((2,)), DMA((2, batches + 1)), DMA((2,)), DMA, DMA((2,)), DMA((2,)), DMA, DMA,
     ]

time: 79.1 us -> 78.4 us (level)
  no operation moved by 1% of the time
where the time goes in v7:
time: 78.4 us; the launch traced here: 78.3 us
  Pallas kernels  77.5 us (99%)
  local copies, waits for them, and re-layouts  0.8 us (1%)
    pallas_call x1, Pallas kernels, shards(): pl.pallas_call(functools.partial(kernel, ny, nd), out_shape=pltpu.VMEM((F...  77.5 us

profile of v7, /device:TPU:37, one launch (start us, length us, event | category | flops | bytes accessed | tf_op | source)
XLA Modules:
  0.0 78.3 jit_solution(8572689258494784848)
XLA Ops:
  0.0 77.5 %decode.1 = bf16[4,32,4,512]{3,2,1,0:T(4,128)(2,1)S(1)} custom-call(bf16[128,512]{1,0:T(8,128)(2,1)} %h_ref.1, bf16[3,9,8,512]{3,2,1,0:T(8,128)(2,1)} %bitcast.4, f32[4,1,128]{2,1,0:T(1,128)} %bitcast.5, f32[4,1,128]{2,1,0:T(1,128)} %bitcast.6, bf16[4,128]{1,0:T(4,128)(2,1)} %bitcast.7), custom_call_target="tpu_custom_call" | custom-call | tf_op jit(solution)/shard_map/decode/pallas_call | solution.py:628
  77.5 0.8 %copy.7 = bf16[4,32,4,512]{3,2,1,0:T(4,128)(2,1)} copy(bf16[4,32,4,512]{3,2,1,0:T(4,128)(2,1)S(1)} %decode.1) | data formatting | bytes 1048576

commit v8 on v7

--- a/solution.py
+++ b/solution.py
@@ -101,7 +101,7 @@
     half = nz // 2
     q, others, group_at = team(ny)
     leaps = (half - NEAR) // 2
-    assert NEAR + 2 * leaps == half
+    assert NEAR + 2 * leaps == half and leaps > 0
     rounds = rounds_of(half)
     spans, last = [], 0
     for known in [1] + [r[1] for r in rounds]:
@@ -222,11 +222,6 @@
             m = w.at[j, me]
             first(m, j)
             remote(m, m, give, giverecv.at[half], sibling).start()
-        for j in range(3):
-            theirs = w.at[j, z * 2]
-            remote(theirs, theirs, own.at[0, 1 + j], own.at[1, 1 + j], sibling).wait_recv()
-        blend(z)
-
         def take(way, d, j, s, on):
             p = piece(z - d if way == 0 else z + d, j)
             hop(way, p, d, j).wait_recv()
@@ -241,6 +236,11 @@
                 take(1, s + 1, j, s, (1,))
             blend(z - s - 1)
             blend(z + s + 1)
+
+        for j in range(3):
+            theirs = w.at[j, z * 2]
+            remote(theirs, theirs, own.at[0, 1 + j], own.at[1, 1 + j], sibling).wait_recv()
+        blend(z)
 
         @pl.loop(0, leaps - 1)
         def _(u):
@@ -282,9 +282,15 @@
         activate((2, 3))
         arrange()
         d, s = half - 2, NEAR - 2 + leaps
-        for j in range(3):
-            take(0, d, j, s, (2,) if j < 2 else ())
-            take(1, d, j, s, () if j < 2 else (2,))
+        def side(way, zz):
+            return w.at[1, pl.ds(lax.rem(zz + 2 * nz, nz) * 2, 2), pl.ds(0, 5) if way == 0 else pl.ds(5, 4)]
+
+        for j in range(3):
+            take(0, d, j, s, (2,) if j == 0 else ())
+            take(1, d, j, s, (2,) if j == 2 else ())
+            if j == 1:
+                hop(0, side(0, z - d), half, j, 2).start()
+                hop(1, side(1, z + d), half, j, 2).start()
         for j in range(3):
             hop(0, piece(z - d, j), d + 1, j).start()
             hop(1, piece(z + d, j), d + 1, j).start()
@@ -303,8 +309,12 @@
             take(1, half - 1, j, s, ())
         blend(z - half + 1)
         blend(z + half - 1)
-        for j in range(3):
-            take(0 if j < 2 else 1, half, j, s, ())
+        take(0, half, 0, s + 1, ())
+        for way in (0, 1):
+            part = side(way, z + half)
+            hop(way, part, half, 1).wait_recv()
+            remote(part, part, give, giverecv.at[s + 1], sibling).start()
+        take(1, half, 2, s + 1, ())
         blend(z + half)
 
     @pl.when(c == 0)
@@ -525,9 +535,10 @@
                 def _():
                     multiply(ROWS // 2, ROWS // 2, 0)
 
-        wait_bytes(w.at[:, pl.ds(0, 6)], giverecv.at[NEAR - 1 + leaps])
+        wait_bytes(w.at[:, pl.ds(0, 4)], giverecv.at[NEAR - 1 + leaps])
         blend(z - half + 1)
         blend(z + half - 1)
+        wait_bytes(w.at[:, pl.ds(0, 2)], giverecv.at[NEAR + leaps])
         blend(z + half)
 
     frame = lax.broadcasted_iota(jnp.int32, (8, LANES), 0) % FRAMES
@@ -560,9 +571,10 @@
     def _():
         wait_bytes(raw.at[0], own.at[0, 0])
         wait_bytes(w.at[:, pl.ds(0, 2 * half - 2)], ringsend.at[0])
-        wait_bytes(w.at[0, pl.ds(0, 1)], ringsend.at[0])
+        wait_bytes(w.at[0, pl.ds(0, 1), pl.ds(0, 1)], ringsend.at[0])
         wait_bytes(w.at[:, pl.ds(0, 2 * half - 3)], ringsend.at[1])
         wait_bytes(w.at[0, pl.ds(0, 2)], ringsend.at[1])
+        wait_bytes(w.at[0, pl.ds(0, 2), pl.ds(0, 4)], ringsend.at[1])
         wait_bytes(w.at[:, pl.ds(0, nd - 1)], give)
 
     @pl.when(c == 0)

time: 78.4 us -> 78.3 us (level)
  no operation moved by 1% of the time
where the time goes in v8:
time: 78.3 us; the launch traced here: 78 us
  Pallas kernels  77.2 us (99%)
  local copies, waits for them, and re-layouts  0.8 us (1%)
    pallas_call x1, Pallas kernels, shards(): pl.pallas_call(functools.partial(kernel, ny, nd), out_shape=pltpu.VMEM((F...  77.2 us

profile of v8, /device:TPU:37, one launch (start us, length us, event | category | flops | bytes accessed | tf_op | source)
XLA Modules:
  0.0 78.0 jit_solution(1865007656563970796)
XLA Ops:
  0.0 77.2 %decode.1 = bf16[4,32,4,512]{3,2,1,0:T(4,128)(2,1)S(1)} custom-call(bf16[128,512]{1,0:T(8,128)(2,1)} %h_ref.1, bf16[3,9,8,512]{3,2,1,0:T(8,128)(2,1)} %bitcast.4, f32[4,1,128]{2,1,0:T(1,128)} %bitcast.5, f32[4,1,128]{2,1,0:T(1,128)} %bitcast.6, bf16[4,128]{1,0:T(4,128)(2,1)} %bitcast.7), custom_call_target="tpu_custom_call" | custom-call | tf_op jit(solution)/shard_map/decode/pallas_call | solution.py:640
  77.2 0.8 %copy.7 = bf16[4,32,4,512]{3,2,1,0:T(4,128)(2,1)} copy(bf16[4,32,4,512]{3,2,1,0:T(4,128)(2,1)S(1)} %decode.1) | data formatting | bytes 1048576
